TPU v7x, 32 devices: a whole 2x2x4 slice. The times are simulated.
32 devices in a mesh: blk: 16 (over z, x, core), dp: 2 (over y).
Axes of the slice: x: 2, y: 2, z: 4, core: 2. Of those that a mesh axis runs over, the one named last changes fastest.
Arguments:
- inputs: bfloat16 [4096, 1024], P(('blk', 'dp')), may hold values from -6 to 6
- cotangent: bfloat16 [4096, 1024], P(('blk', 'dp')), may hold values from -2.5 to 2.5
- task_ids: int32 [4096], P(('blk', 'dp')), may hold values from 0 to 3
- group_counts: int32 [32, 8], P(('blk', 'dp')), may hold values from 1 to 16, as said below
- task_gate: float32 [4, 16], replicated, may hold values from 0.25 to 2
- w_in: bfloat16 [16, 1024, 2048], P('blk'), may hold values from -0.1875 to 0.1875
- w_out: bfloat16 [16, 2048, 1024], P('blk'), may hold values from -0.125 to 0.125
Outputs:
- input_grad: float32 [4096, 1024], P(('blk', 'dp'))
- grad_in: float32 [16, 1024, 2048], P('blk', 'dp')
- grad_out: float32 [16, 2048, 1024], P('blk', 'dp')
Inputs may be any that keep to these rules, and one draw needn't show every extreme that they name: `group_counts`: in every draw one group has all 16 slots live on every device; the others vary from device to device.
All inputs are finite; a program needn't handle non-finite values.
Results may differ from a plain program's by a relative error of at most 0.0042.
Values may be sent and summed in bfloat16 or wider, within the bound.
No kernel may reach another device: no remote copies, remote signals or barrier semaphores. Data moves between devices by JAX's collectives and lax.ppermute only.
A program may use at most 128 MiB of HBM per device.

v0:
```python
import functools

import jax
import jax.numpy as jnp
from jax import lax
from jax.experimental import pallas as pl
from jax.experimental.pallas import tpu as pltpu
from jax.sharding import Mesh
from jax.sharding import PartitionSpec as P


grad_scale = 0.0625
lanes = 128
own_tile = 256
rest_tile = 512
kernel_grant = 48 << 20


smem_spec = pl.BlockSpec(memory_space=pltpu.SMEM)
vmem_spec = pl.BlockSpec(memory_space=pltpu.VMEM)
hbm_spec = pl.BlockSpec(memory_space=pltpu.HBM)
any_spec = pl.BlockSpec(memory_space=pl.ANY)


def contract(left, right, left_dim, right_dim):
    return lax.dot_general(
        left, right, (((left_dim,), (right_dim,)), ((), ())), preferred_element_type=jnp.float32
    )


def partner_of(group, step, groups):
    if groups & (groups - 1) == 0:
        return group ^ step
    return (group + step) % groups


def partner(group, step, groups, sign):
    if groups & (groups - 1) == 0:
        return group ^ step
    return lax.rem(group + sign * step + groups, groups)


def pack_kernel(repeats, groups, capacity, ids, counts, table, x_ref, cot_ref, *outs):
    all_ref, near_refs = outs[0], outs[1:]
    model_width = x_ref.shape[1]
    task_count = table.shape[0]
    own_repeat = lax.axis_index("rep")
    own_group = lax.axis_index("grp")
    row = lax.broadcasted_iota(jnp.int32, (capacity, lanes), 0)
    for step in range(groups):
        group = partner(own_group, step, groups, 1)
        start = pl.multiple_of(group * capacity, capacity)
        live = counts[0, group]
        tags = jnp.full((capacity, lanes), task_count, jnp.int32)
        for slot in range(capacity):
            tags = jnp.where(row == slot, ids[start + slot], tags)
        tags = jnp.where(row < live, tags, task_count)
        rows = pl.ds(start, capacity)
        for hop in range(repeats):
            expert = lax.rem(own_repeat + hop, repeats) * groups + group
            block_refs = [all_ref.at[expert]]
            if hop == 0 and near_refs:
                block_refs.append(near_refs[step])
            gate = jnp.zeros((capacity, lanes), jnp.float32)
            for task in range(task_count):
                gate = jnp.where(tags == task, table[task, expert], gate)
            for ref in block_refs:
                ref[:, :model_width] = x_ref[rows, :]
            for column in range(0, model_width, lanes):
                part = cot_ref[rows, column : column + lanes].astype(jnp.float32) * gate
                part = part.astype(jnp.bfloat16)
                for ref in block_refs:
                    ref[:, model_width + column : model_width + column + lanes] = part


def pack_blocks(sizes, task_ids, group_counts, task_gate, inputs, cotangent):
    repeats, groups, halves, capacity = sizes
    width = 2 * inputs.shape[1]
    near_count = groups if halves > 1 else 0
    out_shape = [jax.ShapeDtypeStruct((repeats * groups, capacity, width), jnp.bfloat16)]
    out_shape += [jax.ShapeDtypeStruct((capacity, width), jnp.bfloat16)] * near_count
    outs = pl.pallas_call(
        functools.partial(pack_kernel, repeats, groups, capacity),
        out_shape=out_shape,
        in_specs=[smem_spec, smem_spec, smem_spec, vmem_spec, vmem_spec],
        out_specs=[vmem_spec] * len(out_shape),
        name="pack_blocks",
    )(task_ids, group_counts, task_gate, inputs, cotangent)
    return outs[0], outs[1:]


def weight_copies(tile, first_hbm, second_hbm, first_ref, second_ref, sems):
    copies = []
    for index in range(first_ref.shape[1] // tile):
        part = slice(index * tile, (index + 1) * tile)
        copies.append(
            (
                pltpu.make_async_copy(
                    first_hbm.at[:, part], first_ref.at[:, part], sems.at[2 * index]
                ),
                pltpu.make_async_copy(
                    second_hbm.at[part, :], second_ref.at[part, :], sems.at[2 * index + 1]
                ),
            )
        )
    for pair in copies:
        for copy in pair:
            copy.start()
    return copies


def wait_pair(pair):
    for copy in pair:
        copy.wait()


def weight_scratch(first_weight, second_weight, tile):
    return [
        pltpu.VMEM(first_weight.shape, first_weight.dtype),
        pltpu.VMEM(second_weight.shape, second_weight.dtype),
        pltpu.SemaphoreType.DMA((2 * first_weight.shape[1] // tile,)),
    ]


def hidden_chunk(x_rows, scaled_cot, first, second):
    pre_act = contract(x_rows, first, 1, 0)
    hidden_cot = contract(scaled_cot, second, 1, 1)
    sigmoid_act = 1.0 / (1.0 + jnp.exp(-pre_act))
    value = pre_act * sigmoid_act
    slope = sigmoid_act * (1.0 + pre_act - value)
    return value.astype(jnp.bfloat16), (hidden_cot * slope).astype(jnp.bfloat16)


def own_kernel(repeats, after_count, rows_ref, first_hbm, second_hbm, *refs):
    act_ref, pre_ref, grad_ref, far_ref, first_ref, second_ref, sems = refs[after_count:]
    row_count = rows_ref.shape[0]
    model_width, hidden_width = first_ref.shape
    copies = weight_copies(own_tile, first_hbm, second_hbm, first_ref, second_ref, sems)
    per_repeat = row_count // repeats
    own_repeat = lax.axis_index("rep")
    for hop in range(1, repeats):
        source = lax.rem(own_repeat + hop, repeats)
        start = pl.multiple_of(source * per_repeat, per_repeat)
        far_ref[hop - 1] = rows_ref[pl.ds(start, per_repeat), :]
    x_rows = rows_ref[:, :model_width]
    scaled_cot = rows_ref[:, model_width:]
    for index, start in enumerate(range(0, hidden_width, own_tile)):
        columns = slice(start, start + own_tile)
        wait_pair(copies[index])
        act, pre = hidden_chunk(x_rows, scaled_cot, first_ref[:, columns], second_ref[columns, :])
        act_ref[:, columns] = act
        pre_ref[:, columns] = pre
    grad_ref[...] = contract(pre_ref[...], first_ref[...], 1, 1).astype(jnp.bfloat16)


def own_parts(repeats, rows, first_weight, second_weight, after):
    row_count, width = rows.shape
    model_width, hidden_width = first_weight.shape
    wide = jax.ShapeDtypeStruct((row_count, hidden_width), jnp.bfloat16)
    return pl.pallas_call(
        functools.partial(own_kernel, repeats, len(after)),
        out_shape=[
            wide,
            wide,
            jax.ShapeDtypeStruct((row_count, model_width), jnp.bfloat16),
            jax.ShapeDtypeStruct((repeats - 1, row_count // repeats, width), jnp.bfloat16),
        ],
        in_specs=[vmem_spec, any_spec, any_spec] + [any_spec] * len(after),
        out_specs=[vmem_spec] * 4,
        scratch_shapes=weight_scratch(first_weight, second_weight, own_tile),
        compiler_params=pltpu.CompilerParams(vmem_limit_bytes=kernel_grant),
        cost_estimate=pl.CostEstimate(
            flops=6 * row_count * model_width * hidden_width,
            bytes_accessed=4 * model_width * hidden_width,
            transcendentals=0,
        ),
        name="own_parts",
    )(rows, first_weight, second_weight, *after)


def rest_kernel(other_count, own_ref, act_ref, pre_ref, *refs):
    other_refs = refs[:other_count]
    first_hbm, second_hbm, first_out, second_out = refs[other_count : other_count + 4]
    other, other_act, left, first_buf, second_buf, sems = refs[other_count + 4 : other_count + 10]
    first_ref, second_ref, weight_sems = refs[other_count + 10 :]
    loads = weight_copies(rest_tile, first_hbm, second_hbm, first_ref, second_ref, weight_sems)
    own_count = own_ref.shape[0]
    model_width, _ = first_ref.shape
    first_tiles, first_rows, first_tile = first_buf.shape
    second_tiles, second_tile, _ = second_buf.shape
    half = lax.axis_index("dp")
    place = 0
    for ref in other_refs:
        other[place : place + ref.shape[0], :] = ref[...]
        place += ref.shape[0]
    x_begin = pl.multiple_of(half * first_rows, first_rows)
    left[:, :own_count] = own_ref[:, pl.ds(x_begin, first_rows)].T
    left[:, own_count:] = other[:, pl.ds(x_begin, first_rows)].T
    copies = []
    for tile in range(first_tiles):
        columns = slice(tile * first_tile, (tile + 1) * first_tile)
        wait_pair(loads[tile])
        act, pre = hidden_chunk(
            other[:, :model_width],
            other[:, model_width:],
            first_ref[:, columns],
            second_ref[columns, :],
        )
        other_act[:, columns] = act
        total = contract(left[:, :own_count], pre_ref[:, columns], 1, 0)
        total += contract(left[:, own_count:], pre, 1, 0)
        first_buf[tile] = total * grad_scale
        if copies:
            copies[-1].start()
        copies.append(
            pltpu.make_async_copy(first_buf.at[tile], first_out.at[:, columns], sems.at[tile])
        )
    for tile in range(second_tiles):
        begin = half * (second_tiles * second_tile) + tile * second_tile
        columns = pl.ds(pl.multiple_of(begin, second_tile), second_tile)
        total = contract(act_ref[:, columns].T, own_ref[:, model_width:], 1, 0)
        total += contract(other_act[:, columns].T, other[:, model_width:], 1, 0)
        second_buf[tile] = total * grad_scale
        copies[-1].start()
        rows = slice(tile * second_tile, (tile + 1) * second_tile)
        copies.append(
            pltpu.make_async_copy(
                second_buf.at[tile], second_out.at[rows, :], sems.at[first_tiles + tile]
            )
        )
    copies[-1].start()
    for copy in copies:
        copy.wait()


def rest_parts(halves, own, act, pre, others, first_weight, second_weight):
    own_count, width = own.shape
    model_width, hidden_width = first_weight.shape
    other_rows = sum(part.shape[0] for part in others)
    first_rows, second_rows = model_width // halves, hidden_width // halves
    first_tiles = hidden_width // rest_tile
    second_tiles = second_rows // rest_tile
    row_count = own_count + other_rows
    flops = 4 * (row_count * first_rows + other_rows * model_width) * hidden_width
    return pl.pallas_call(
        functools.partial(rest_kernel, len(others)),
        out_shape=[
            jax.ShapeDtypeStruct((first_rows, hidden_width), jnp.float32),
            jax.ShapeDtypeStruct((second_rows, model_width), jnp.float32),
        ],
        in_specs=[vmem_spec] * (3 + len(others)) + [any_spec] * 2,
        out_specs=[hbm_spec, hbm_spec],
        scratch_shapes=[
            pltpu.VMEM((other_rows, width), jnp.bfloat16),
            pltpu.VMEM((other_rows, hidden_width), jnp.bfloat16),
            pltpu.VMEM((first_rows, row_count), jnp.bfloat16),
            pltpu.VMEM((first_tiles, first_rows, rest_tile), jnp.float32),
            pltpu.VMEM((second_tiles, rest_tile, model_width), jnp.float32),
            pltpu.SemaphoreType.DMA((first_tiles + second_tiles,)),
            *weight_scratch(first_weight, second_weight, rest_tile),
        ],
        compiler_params=pltpu.CompilerParams(vmem_limit_bytes=kernel_grant),
        cost_estimate=pl.CostEstimate(
            flops=flops, bytes_accessed=8 * first_rows * hidden_width, transcendentals=0
        ),
        name="rest_parts",
    )(own, act, pre, *others, first_weight, second_weight)


def on_device(inputs, cotangent, task_ids, group_counts, task_gate, w_in, w_out):
    groups = group_counts.shape[1]
    model_width = inputs.shape[1]
    capacity = inputs.shape[0] // groups
    repeats = lax.axis_size("rep")
    halves = lax.axis_size("dp")
    first_weight = w_in[0]
    second_weight = w_out[0]
    outgoing, near = pack_blocks(
        (repeats, groups, halves, capacity), task_ids, group_counts, task_gate, inputs, cotangent
    )
    width = outgoing.shape[-1]

    def across(turn, step):
        pairs = []
        for source in range(groups * halves):
            group, half = divmod(source, halves)
            target = partner_of(group, step, groups) * halves + (half + turn) % halves
            pairs.append((source, target))
        return pairs

    own_rows = lax.all_to_all(outgoing, ("rep", "grp"), 0, 0)
    near_other = [
        lax.ppermute(near[step], ("grp", "dp"), across(turn, step))
        for turn in range(1, halves)
        for step in range(groups)
    ]
    own = own_rows.reshape(repeats * groups * capacity, width)
    act, pre, row_grads, far_rows = own_parts(repeats, own, first_weight, second_weight, [])
    far_other = []
    for hop in range(repeats - 1):
        for turn in range(1, halves):
            pairs = [(i, (i + turn) % halves) for i in range(halves)]
            far_other.append(lax.ppermute(far_rows[hop], "dp", pairs))
    returned = lax.all_to_all(
        row_grads.reshape(repeats * groups, capacity, model_width), ("rep", "grp"), 0, 0
    )
    grad_first, grad_second = rest_parts(
        halves, own, act, pre, near_other + far_other, first_weight, second_weight
    )
    input_home = jnp.sum(
        returned.reshape(repeats, groups * capacity, model_width).astype(jnp.float32), axis=0
    )
    return (input_home, grad_first[None], grad_second[None])


def solution(mesh):

    def step(inputs, cotangent, task_ids, group_counts, task_gate, w_in, w_out):
        groups = group_counts.shape[1]
        halves = mesh.shape["dp"]
        repeats = mesh.shape["blk"] // groups
        fine = Mesh(mesh.devices.reshape(repeats, groups, halves), ("rep", "grp", "dp"))
        rows = P(("rep", "grp", "dp"))
        expert = P(("rep", "grp"))
        split = P(("rep", "grp"), "dp")
        return jax.shard_map(
            on_device,
            mesh=fine,
            in_specs=(rows, rows, rows, rows, P(), expert, expert),
            out_specs=(rows, split, split),
            check_vma=False,
        )(inputs, cotangent, task_ids, group_counts, task_gate, w_in, w_out)

    return step
```

profile of v0, /device:TPU:1, one launch (start us, length us, event | category | flops | bytes accessed | tf_op | source)
XLA Modules:
  0.0 90.6 jit_solution(5514664341080764878)
XLA Ops:
  0.6 2.4 %pack_blocks.1 = (bf16[16,16,2048]{2,1,0:T(8,128)(2,1)}, bf16[16,2048]{1,0:T(8,128)(2,1)}, bf16[16,2048]{1,0:T(8,128)(2,1)}, bf16[16,2048]{1,0:T(8,128)(2,1)}, b...) custom-call(s32[128]{0:T(128)} %ids.1, ...), custom_call_target="tpu_custom_call" | custom-call | tf_op jit(solution)/shard_map/pack_blocks/pallas_call | solution.py:82
  3.0 32.6 %all_to_all.10 = bf16[16,16,2048]{2,1,0:T(8,128)(2,1)S(1)} all-to-all(bf16[16,16,2048]{2,1,0:T(8,128)(2,1)} %get-tuple-element.18), channel_id=1, replica_groups=mesh['rep'=2,'grp'=8,'dp'=2] {'rep','grp'}, dimensions={0} | all-to-all | bytes 2097152 | tf_op jit(solution)/shard_map/all_to_all | solution.py:291
  35.6 7.1 %own_parts.1 = (bf16[256,2048]{1,0:T(8,128)(2,1)S(1)}, bf16[256,2048]{1,0:T(8,128)(2,1)S(1)}, bf16[256,1024]{1,0:T(8,128)(2,1)}, bf16[1,128,2048]{2,1,0:T(8,128)(2,1)S(1)}) custom-call(bf16[256,2048]{1,0:T(8,128)(2,1)S(1)} %bitcast.11, bf16[1024,2048]{1,0:T(8,128)(2,1)} %bitcast.15, bf16[2048,1024]{1,0:T(8,128)(2,1)} %bitcast.17), custom_call_target="tpu_custom_call" | custom-call | flops 3221225472 | bytes 8388608 | tf_op jit(solution)/shard_map/own_parts/pallas_call | solution.py:160
  42.8 0.0 copy-start
  42.8 1.0 %copy-done = bf16[256,2048]{1,0:T(8,128)(2,1)} copy-done((bf16[256,2048]{1,0:T(8,128)(2,1)}, bf16[256,2048]{1,0:T(8,128)(2,1)S(1)}, u32[]{:S(2)}) %copy-start) | copy-done | bytes 1048600
  43.7 4.5 %all-to-all-start.1 = ((bf16[16,16,1024]{2,1,0:T(8,128)(2,1)}), bf16[16,16,1024]{2,1,0:T(8,128)(2,1)S(1)}, u32[]{:S(2)}, u32[]{:S(2)}) async-start(bf16[16,16,1024]{2,1,0:T(8,128)(2,1)} %bitcast.3), calls=%async_computation.1 | async-start | bytes 1048576 | tf_op jit(solution)/shard_map/all_to_all | solution.py:304
  48.2 1.2 %collective-permute-start.8 = (bf16[128,2048]{1,0:T(8,128)(2,1)S(1)}, bf16[128,2048]{1,0:T(8,128)(2,1)S(1)}, u32[]{:S(2)}, u32[]{:S(2)}) collective-permute-start(bf16[128,2048]{1,0:T(8,128)(2,1)S(1)} %bitcast.13), channel_id=1, source_target_pairs={{0,1},{1,0},{2,3},{3,2},{4,5},{5,4},{6,7},{7,6},{8,9},{9,8},{10,11... | collective-permute-start | bytes 1572872 | tf_op jit(solution)/shard_map/ppermute | solution.py:303
  49.4 0.2 collective-permute-start
  49.7 1.8 %collective-permute-start.1 = (bf16[16,2048]{1,0:T(8,128)(2,1)}, bf16[16,2048]{1,0:T(8,128)(2,1)S(1)}, u32[]{:S(2)}, u32[]{:S(2)}) collective-permute-start(bf16[16,2048]{1,0:T(8,128)(2,1)} %get-tuple-element.23), channel_id=1, source_target_pairs={{0,3},{1,2},{2,1},{3,0},{4,7},{5,6},{6,5},{7,4},{8,11},{9,10},{10,... | collective-permute-start | bytes 196616 | tf_op jit(solution)/shard_map/ppermute | solution.py:293
  51.5 1.5 %collective-permute-start.2 = (bf16[16,2048]{1,0:T(8,128)(2,1)S(1)}, bf16[16,2048]{1,0:T(8,128)(2,1)S(1)}, u32[]{:S(2)}, u32[]{:S(2)}) collective-permute-start(bf16[16,2048]{1,0:T(8,128)(2,1)S(1)} %copy-done.7), channel_id=1, source_target_pairs={{0,5},{1,4},{2,7},{3,6},{4,1},{5,0},{6,3},{7,2},{8,13},{9,12},{10,... | collective-permute-start | bytes 196616 | tf_op jit(solution)/shard_map/ppermute | solution.py:293
  53.0 0.8 collective-permute-start.3
  53.8 11.9 %collective-permute-done.refs_0_ = bf16[16,2048]{1,0:T(8,128)(2,1)S(1)} collective-permute-done((bf16[16,2048]{1,0:T(8,128)(2,1)}, bf16[16,2048]{1,0:T(8,128)(2,1)S(1)}, u32[]{:S(2)}, u32[]{:S(2)}) %collective-permute-start) | collective-permute-done | bytes 65568 | tf_op jit(solution)/shard_map/ppermute | solution.py:293
  65.7 2.1 %collective-permute-start.4 = (bf16[16,2048]{1,0:T(8,128)(2,1)S(1)}, bf16[16,2048]{1,0:T(8,128)(2,1)S(1)}, u32[]{:S(2)}, u32[]{:S(2)}) collective-permute-start(bf16[16,2048]{1,0:T(8,128)(2,1)S(1)} %copy-done.5), channel_id=1, source_target_pairs={{0,9},{1,8},{2,11},{3,10},{4,13},{5,12},{6,15},{7,14},{8,1},{9,0},... | collective-permute-start | bytes 196616 | tf_op jit(solution)/shard_map/ppermute | solution.py:293
  67.8 0.0 collective-permute-done.1.refs_1_
  67.8 2.1 %collective-permute-start.5 = (bf16[16,2048]{1,0:T(8,128)(2,1)S(1)}, bf16[16,2048]{1,0:T(8,128)(2,1)S(1)}, u32[]{:S(2)}, u32[]{:S(2)}) collective-permute-start(bf16[16,2048]{1,0:T(8,128)(2,1)S(1)} %copy-done.4), channel_id=1, source_target_pairs={{0,11},{1,10},{2,9},{3,8},{4,15},{5,14},{6,13},{7,12},{8,3},{9,2},... | collective-permute-start | bytes 196616 | tf_op jit(solution)/shard_map/ppermute | solution.py:293
  69.9 0.0 collective-permute-done.2.refs_2_
  69.9 3.3 %collective-permute-start.6 = (bf16[16,2048]{1,0:T(8,128)(2,1)S(1)}, bf16[16,2048]{1,0:T(8,128)(2,1)S(1)}, u32[]{:S(2)}, u32[]{:S(2)}) collective-permute-start(bf16[16,2048]{1,0:T(8,128)(2,1)S(1)} %copy-done.3), channel_id=1, source_target_pairs={{0,13},{1,12},{2,15},{3,14},{4,9},{5,8},{6,11},{7,10},{8,5},{9,4},... | collective-permute-start | bytes 196616 | tf_op jit(solution)/shard_map/ppermute | solution.py:293
  73.2 0.4 collective-permute-start.7
  73.6 0.0 collective-permute-done.4.refs_4_
  73.6 2.9 %collective-permute-done.6.refs_6_ = bf16[16,2048]{1,0:T(8,128)(2,1)S(1)} collective-permute-done((bf16[16,2048]{1,0:T(8,128)(2,1)S(1)}, bf16[16,2048]{1,0:T(8,128)(2,1)S(1)}, u32[]{:S(2)}, u32[]{:S(2)}) %collective-permute-start.6) | collective-permute-done | bytes 65568 | tf_op jit(solution)/shard_map/ppermute | solution.py:293
  76.5 2.2 %collective-permute-done.7.refs_7_ = bf16[16,2048]{1,0:T(8,128)(2,1)S(1)} collective-permute-done((bf16[16,2048]{1,0:T(8,128)(2,1)S(1)}, bf16[16,2048]{1,0:T(8,128)(2,1)S(1)}, u32[]{:S(2)}, u32[]{:S(2)}) %collective-permute-start.7) | collective-permute-done | bytes 65568 | tf_op jit(solution)/shard_map/ppermute | solution.py:293
  78.7 1.2 %copy-done.1 = bf16[256,2048]{1,0:T(8,128)(2,1)S(1)} copy-done((bf16[256,2048]{1,0:T(8,128)(2,1)S(1)}, bf16[256,2048]{1,0:T(8,128)(2,1)}, u32[]{:S(2)}) %copy-start.1) | copy-done | bytes 1048600
  79.9 9.7 %rest_parts.1 = (f32[512,2048]{1,0:T(8,128)}, f32[1024,1024]{1,0:T(8,128)}) custom-call(bf16[256,2048]{1,0:T(8,128)(2,1)S(1)} %bitcast.12, bf16[256,2048]{1,0:T(8,128)(2,1)S(1)} %get-tuple-element.20.act_ref, bf16[256,2048]{1,0:T(8,128)(2,1)S(1)} %copy-done.1, bf16[16,2048]{1,0:T(8,128)(2,1)S(1)} %collective-permute-done.refs_0_, ...), custom_call_target="tpu_custom_call" | custom-call | flops 4294967296 | bytes 8388608 | tf_op jit(solution)/shard_map/rest_parts/pallas_call | solution.py:245
  89.7 0.9 convert_reduce_fusion
  (17 shorter events, 0.0 us)
Async XLA Ops:
  35.6 15.9 %copy-start.7 = (bf16[16,2048]{1,0:T(8,128)(2,1)S(1)}, bf16[16,2048]{1,0:T(8,128)(2,1)}, u32[]{:S(2)}) copy-start(bf16[16,2048]{1,0:T(8,128)(2,1)} %get-tuple-element.24) | copy-start | bytes 196612
  35.6 17.4 %copy-start.6 = (bf16[16,2048]{1,0:T(8,128)(2,1)S(1)}, bf16[16,2048]{1,0:T(8,128)(2,1)}, u32[]{:S(2)}) copy-start(bf16[16,2048]{1,0:T(8,128)(2,1)} %get-tuple-element.25) | copy-start | bytes 196612
  35.6 30.1 %copy-start.5 = (bf16[16,2048]{1,0:T(8,128)(2,1)S(1)}, bf16[16,2048]{1,0:T(8,128)(2,1)}, u32[]{:S(2)}) copy-start(bf16[16,2048]{1,0:T(8,128)(2,1)} %get-tuple-element.26) | copy-start | bytes 196612
  35.6 32.2 %copy-start.4 = (bf16[16,2048]{1,0:T(8,128)(2,1)S(1)}, bf16[16,2048]{1,0:T(8,128)(2,1)}, u32[]{:S(2)}) copy-start(bf16[16,2048]{1,0:T(8,128)(2,1)} %get-tuple-element.27) | copy-start | bytes 196612
  35.6 34.3 %copy-start.3 = (bf16[16,2048]{1,0:T(8,128)(2,1)S(1)}, bf16[16,2048]{1,0:T(8,128)(2,1)}, u32[]{:S(2)}) copy-start(bf16[16,2048]{1,0:T(8,128)(2,1)} %get-tuple-element.28) | copy-start | bytes 196612
  35.6 37.6 %copy-start.2 = (bf16[16,2048]{1,0:T(8,128)(2,1)S(1)}, bf16[16,2048]{1,0:T(8,128)(2,1)}, u32[]{:S(2)}) copy-start(bf16[16,2048]{1,0:T(8,128)(2,1)} %get-tuple-element.29) | copy-start | bytes 196612
  42.8 1.0 %copy-start = (bf16[256,2048]{1,0:T(8,128)(2,1)}, bf16[256,2048]{1,0:T(8,128)(2,1)S(1)}, u32[]{:S(2)}) copy-start(bf16[256,2048]{1,0:T(8,128)(2,1)S(1)} %get-tuple-element.21.pre_ref) | copy-start | bytes 3145732
  43.7 46.0 %all-to-all-start.1 = ((bf16[16,16,1024]{2,1,0:T(8,128)(2,1)}), bf16[16,16,1024]{2,1,0:T(8,128)(2,1)S(1)}, u32[]{:S(2)}, u32[]{:S(2)}) async-start(bf16[16,16,1024]{2,1,0:T(8,128)(2,1)} %bitcast.3), calls=%async_computation.1 | async-start | bytes 1048576 | tf_op jit(solution)/shard_map/all_to_all | solution.py:304
  48.2 30.5 %collective-permute-start.8 = (bf16[128,2048]{1,0:T(8,128)(2,1)S(1)}, bf16[128,2048]{1,0:T(8,128)(2,1)S(1)}, u32[]{:S(2)}, u32[]{:S(2)}) collective-permute-start(bf16[128,2048]{1,0:T(8,128)(2,1)S(1)} %bitcast.13), channel_id=1, source_target_pairs={{0,1},{1,0},{2,3},{3,2},{4,5},{5,4},{6,7},{7,6},{8,9},{9,8},{10,11... | collective-permute-start | bytes 1572872 | tf_op jit(solution)/shard_map/ppermute | solution.py:303
  49.4 16.3 %collective-permute-start = (bf16[16,2048]{1,0:T(8,128)(2,1)}, bf16[16,2048]{1,0:T(8,128)(2,1)S(1)}, u32[]{:S(2)}, u32[]{:S(2)}) collective-permute-start(bf16[16,2048]{1,0:T(8,128)(2,1)} %get-tuple-element.22), channel_id=1, source_target_pairs={{0,1},{1,0},{2,3},{3,2},{4,5},{5,4},{6,7},{7,6},{8,9},{9,8},{10,11... | collective-permute-start | bytes 196616 | tf_op jit(solution)/shard_map/ppermute | solution.py:293
  49.7 18.1 %collective-permute-start.1 = (bf16[16,2048]{1,0:T(8,128)(2,1)}, bf16[16,2048]{1,0:T(8,128)(2,1)S(1)}, u32[]{:S(2)}, u32[]{:S(2)}) collective-permute-start(bf16[16,2048]{1,0:T(8,128)(2,1)} %get-tuple-element.23), channel_id=1, source_target_pairs={{0,3},{1,2},{2,1},{3,0},{4,7},{5,6},{6,5},{7,4},{8,11},{9,10},{10,... | collective-permute-start | bytes 196616 | tf_op jit(solution)/shard_map/ppermute | solution.py:293
  51.5 18.4 %collective-permute-start.2 = (bf16[16,2048]{1,0:T(8,128)(2,1)S(1)}, bf16[16,2048]{1,0:T(8,128)(2,1)S(1)}, u32[]{:S(2)}, u32[]{:S(2)}) collective-permute-start(bf16[16,2048]{1,0:T(8,128)(2,1)S(1)} %copy-done.7), channel_id=1, source_target_pairs={{0,5},{1,4},{2,7},{3,6},{4,1},{5,0},{6,3},{7,2},{8,13},{9,12},{10,... | collective-permute-start | bytes 196616 | tf_op jit(solution)/shard_map/ppermute | solution.py:293
  53.0 20.2 %collective-permute-start.3 = (bf16[16,2048]{1,0:T(8,128)(2,1)S(1)}, bf16[16,2048]{1,0:T(8,128)(2,1)S(1)}, u32[]{:S(2)}, u32[]{:S(2)}) collective-permute-start(bf16[16,2048]{1,0:T(8,128)(2,1)S(1)} %copy-done.6), channel_id=1, source_target_pairs={{0,7},{1,6},{2,5},{3,4},{4,3},{5,2},{6,1},{7,0},{8,15},{9,14},{10,... | collective-permute-start | bytes 196616 | tf_op jit(solution)/shard_map/ppermute | solution.py:293
  65.7 7.9 %collective-permute-start.4 = (bf16[16,2048]{1,0:T(8,128)(2,1)S(1)}, bf16[16,2048]{1,0:T(8,128)(2,1)S(1)}, u32[]{:S(2)}, u32[]{:S(2)}) collective-permute-start(bf16[16,2048]{1,0:T(8,128)(2,1)S(1)} %copy-done.5), channel_id=1, source_target_pairs={{0,9},{1,8},{2,11},{3,10},{4,13},{5,12},{6,15},{7,14},{8,1},{9,0},... | collective-permute-start | bytes 196616 | tf_op jit(solution)/shard_map/ppermute | solution.py:293
  67.8 5.8 %collective-permute-start.5 = (bf16[16,2048]{1,0:T(8,128)(2,1)S(1)}, bf16[16,2048]{1,0:T(8,128)(2,1)S(1)}, u32[]{:S(2)}, u32[]{:S(2)}) collective-permute-start(bf16[16,2048]{1,0:T(8,128)(2,1)S(1)} %copy-done.4), channel_id=1, source_target_pairs={{0,11},{1,10},{2,9},{3,8},{4,15},{5,14},{6,13},{7,12},{8,3},{9,2},... | collective-permute-start | bytes 196616 | tf_op jit(solution)/shard_map/ppermute | solution.py:293
  69.9 6.6 %collective-permute-start.6 = (bf16[16,2048]{1,0:T(8,128)(2,1)S(1)}, bf16[16,2048]{1,0:T(8,128)(2,1)S(1)}, u32[]{:S(2)}, u32[]{:S(2)}) collective-permute-start(bf16[16,2048]{1,0:T(8,128)(2,1)S(1)} %copy-done.3), channel_id=1, source_target_pairs={{0,13},{1,12},{2,15},{3,14},{4,9},{5,8},{6,11},{7,10},{8,5},{9,4},... | collective-permute-start | bytes 196616 | tf_op jit(solution)/shard_map/ppermute | solution.py:293
  73.2 5.5 %collective-permute-start.7 = (bf16[16,2048]{1,0:T(8,128)(2,1)S(1)}, bf16[16,2048]{1,0:T(8,128)(2,1)S(1)}, u32[]{:S(2)}, u32[]{:S(2)}) collective-permute-start(bf16[16,2048]{1,0:T(8,128)(2,1)S(1)} %copy-done.2), channel_id=1, source_target_pairs={{0,15},{1,14},{2,13},{3,12},{4,11},{5,10},{6,9},{7,8},{8,7},{9,6},... | collective-permute-start | bytes 196616 | tf_op jit(solution)/shard_map/ppermute | solution.py:293
  78.7 1.2 %copy-start.1 = (bf16[256,2048]{1,0:T(8,128)(2,1)S(1)}, bf16[256,2048]{1,0:T(8,128)(2,1)}, u32[]{:S(2)}) copy-start(bf16[256,2048]{1,0:T(8,128)(2,1)} %copy-done) | copy-start | bytes 3145732
where the time goes:
time: 90.9 us; the launch traced here: 90.6 us
  blocking collectives  32.6 us (36%)
  Pallas kernels  19.3 us (21%)
  starting transfers between devices  18 us (20%)
  waiting for transfers between devices  17 us (19%)
  local copies, waits for them, and re-layouts  2.21 us (2%)
    all_to_all x1, blocking collectives, on_device(): own_rows = lax.all_to_all(outgoing, ('rep', 'grp'), 0, 0)  32.6 us
    ppermute x8, waiting for transfers between devices, on_device(): lax.ppermute(near[step], ('grp', 'dp'), across(turn, step))  17 us
    ppermute x8, starting transfers between devices, on_device(): lax.ppermute(near[step], ('grp', 'dp'), across(turn, step))  12.2 us
    pallas_call x1, Pallas kernels, rest_parts(): pl.pallas_call(functools.partial(rest_kernel, len(others)), out_shape=[ja...  9.73 us
    pallas_call x1, Pallas kernels, own_parts(): pl.pallas_call(functools.partial(own_kernel, repeats, len(after)), out_sh...  7.11 us
    all_to_all x1, starting transfers between devices, on_device(): lax.all_to_all(row_grads.reshape(repeats * groups, capacity, model_width)...  4.48 us
    pallas_call x1, Pallas kernels, pack_blocks(): pl.pallas_call(functools.partial(pack_kernel, repeats, groups, capacity),...  2.42 us
    unnamed x16, local copies, waits for them, and re-layouts  2.21 us
  transfers between devices with their start and end apart: 10, of which 3 were waited for; matrix products, arithmetic and copies ran while one was open for 0% of the time, Pallas kernels for 11%

commit v1 on v0

--- a/solution.py
+++ b/solution.py
@@ -14,6 +14,8 @@
 own_tile = 256
 rest_tile = 512
 kernel_grant = 48 << 20
+load_depth = 4
+stage_grant = 1 << 20
 
 
 smem_spec = pl.BlockSpec(memory_space=pltpu.SMEM)
@@ -103,15 +105,25 @@
                 ),
             )
         )
-    for pair in copies:
-        for copy in pair:
-            copy.start()
+    for pair in copies[:load_depth]:
+        start_pair(pair)
     return copies
+
+
+def start_pair(pair):
+    for copy in pair:
+        copy.start()
 
 
 def wait_pair(pair):
     for copy in pair:
         copy.wait()
+
+
+def next_pair(copies, index):
+    if index + load_depth < len(copies):
+        start_pair(copies[index + load_depth])
+    wait_pair(copies[index])
 
 
 def weight_scratch(first_weight, second_weight, tile):
@@ -131,8 +143,9 @@
     return value.astype(jnp.bfloat16), (hidden_cot * slope).astype(jnp.bfloat16)
 
 
-def own_kernel(repeats, after_count, rows_ref, first_hbm, second_hbm, *refs):
-    act_ref, pre_ref, grad_ref, far_ref, first_ref, second_ref, sems = refs[after_count:]
+def own_kernel(repeats, rows_ref, first_hbm, second_hbm, *refs):
+    act_hbm, pre_hbm, grad_ref, far_ref = refs[:4]
+    act_ref, pre_ref, total_ref, out_sems, first_ref, second_ref, sems = refs[4:]
     row_count = rows_ref.shape[0]
     model_width, hidden_width = first_ref.shape
     copies = weight_copies(own_tile, first_hbm, second_hbm, first_ref, second_ref, sems)
@@ -144,30 +157,57 @@
         far_ref[hop - 1] = rows_ref[pl.ds(start, per_repeat), :]
     x_rows = rows_ref[:, :model_width]
     scaled_cot = rows_ref[:, model_width:]
-    for index, start in enumerate(range(0, hidden_width, own_tile)):
-        columns = slice(start, start + own_tile)
-        wait_pair(copies[index])
+    stores = []
+    last = hidden_width // own_tile - 1
+    for index in range(last + 1):
+        columns = slice(index * own_tile, (index + 1) * own_tile)
+        next_pair(copies, index)
         act, pre = hidden_chunk(x_rows, scaled_cot, first_ref[:, columns], second_ref[columns, :])
         act_ref[:, columns] = act
         pre_ref[:, columns] = pre
-    grad_ref[...] = contract(pre_ref[...], first_ref[...], 1, 1).astype(jnp.bfloat16)
-
-
-def own_parts(repeats, rows, first_weight, second_weight, after):
+        part = contract(pre, first_ref[:, columns], 1, 1)
+        if index == 0:
+            total_ref[...] = part
+        elif index < last:
+            total_ref[...] += part
+        else:
+            grad_ref[...] = (total_ref[...] + part).astype(jnp.bfloat16)
+        stores.append(
+            (
+                pltpu.make_async_copy(
+                    act_ref.at[:, columns], act_hbm.at[:, columns], out_sems.at[2 * index]
+                ),
+                pltpu.make_async_copy(
+                    pre_ref.at[:, columns], pre_hbm.at[:, columns], out_sems.at[2 * index + 1]
+                ),
+            )
+        )
+        start_pair(stores[-1])
+    for pair in stores:
+        wait_pair(pair)
+
+
+def own_parts(repeats, rows, first_weight, second_weight):
     row_count, width = rows.shape
     model_width, hidden_width = first_weight.shape
     wide = jax.ShapeDtypeStruct((row_count, hidden_width), jnp.bfloat16)
     return pl.pallas_call(
-        functools.partial(own_kernel, repeats, len(after)),
+        functools.partial(own_kernel, repeats),
         out_shape=[
             wide,
             wide,
             jax.ShapeDtypeStruct((row_count, model_width), jnp.bfloat16),
             jax.ShapeDtypeStruct((repeats - 1, row_count // repeats, width), jnp.bfloat16),
         ],
-        in_specs=[vmem_spec, any_spec, any_spec] + [any_spec] * len(after),
-        out_specs=[vmem_spec] * 4,
-        scratch_shapes=weight_scratch(first_weight, second_weight, own_tile),
+        in_specs=[vmem_spec, any_spec, any_spec],
+        out_specs=[hbm_spec, hbm_spec, vmem_spec, vmem_spec],
+        scratch_shapes=[
+            pltpu.VMEM(wide.shape, wide.dtype),
+            pltpu.VMEM(wide.shape, wide.dtype),
+            pltpu.VMEM((row_count, model_width), jnp.float32),
+            pltpu.SemaphoreType.DMA((2 * hidden_width // own_tile,)),
+            *weight_scratch(first_weight, second_weight, own_tile),
+        ],
         compiler_params=pltpu.CompilerParams(vmem_limit_bytes=kernel_grant),
         cost_estimate=pl.CostEstimate(
             flops=6 * row_count * model_width * hidden_width,
@@ -175,15 +215,35 @@
             transcendentals=0,
         ),
         name="own_parts",
-    )(rows, first_weight, second_weight, *after)
+    )(rows, first_weight, second_weight)
+
+
+def stage_kernel(count, *refs):
+    sems = refs[-1]
+    copies = [
+        pltpu.make_async_copy(refs[i], refs[count + i], sems.at[i]) for i in range(count)
+    ]
+    start_pair(copies)
+    wait_pair(copies)
+
+
+def stage(arrays):
+    count = len(arrays)
+    return pl.pallas_call(
+        functools.partial(stage_kernel, count),
+        out_shape=[jax.ShapeDtypeStruct(part.shape, part.dtype) for part in arrays],
+        in_specs=[any_spec] * count,
+        out_specs=[any_spec] * count,
+        scratch_shapes=[pltpu.SemaphoreType.DMA((count,))],
+        compiler_params=pltpu.CompilerParams(vmem_limit_bytes=stage_grant),
+        name="stage",
+    )(*arrays)
 
 
 def rest_kernel(other_count, own_ref, act_ref, pre_ref, *refs):
     other_refs = refs[:other_count]
-    first_hbm, second_hbm, first_out, second_out = refs[other_count : other_count + 4]
-    other, other_act, left, first_buf, second_buf, sems = refs[other_count + 4 : other_count + 10]
-    first_ref, second_ref, weight_sems = refs[other_count + 10 :]
-    loads = weight_copies(rest_tile, first_hbm, second_hbm, first_ref, second_ref, weight_sems)
+    first_ref, second_ref, first_out, second_out = refs[other_count : other_count + 4]
+    other, other_act, left, first_buf, second_buf, sems = refs[other_count + 4 :]
     own_count = own_ref.shape[0]
     model_width, _ = first_ref.shape
     first_tiles, first_rows, first_tile = first_buf.shape
@@ -199,7 +259,6 @@
     copies = []
     for tile in range(first_tiles):
         columns = slice(tile * first_tile, (tile + 1) * first_tile)
-        wait_pair(loads[tile])
         act, pre = hidden_chunk(
             other[:, :model_width],
             other[:, model_width:],
@@ -248,7 +307,7 @@
             jax.ShapeDtypeStruct((first_rows, hidden_width), jnp.float32),
             jax.ShapeDtypeStruct((second_rows, model_width), jnp.float32),
         ],
-        in_specs=[vmem_spec] * (3 + len(others)) + [any_spec] * 2,
+        in_specs=[vmem_spec] * (5 + len(others)),
         out_specs=[hbm_spec, hbm_spec],
         scratch_shapes=[
             pltpu.VMEM((other_rows, width), jnp.bfloat16),
@@ -257,9 +316,10 @@
             pltpu.VMEM((first_tiles, first_rows, rest_tile), jnp.float32),
             pltpu.VMEM((second_tiles, rest_tile, model_width), jnp.float32),
             pltpu.SemaphoreType.DMA((first_tiles + second_tiles,)),
-            *weight_scratch(first_weight, second_weight, rest_tile),
         ],
-        compiler_params=pltpu.CompilerParams(vmem_limit_bytes=kernel_grant),
+        compiler_params=pltpu.CompilerParams(
+            vmem_limit_bytes=min(60 << 20, (16 << 20) + row_count * (32 << 10))
+        ),
         cost_estimate=pl.CostEstimate(
             flops=flops, bytes_accessed=8 * first_rows * hidden_width, transcendentals=0
         ),
@@ -295,7 +355,7 @@
         for step in range(groups)
     ]
     own = own_rows.reshape(repeats * groups * capacity, width)
-    act, pre, row_grads, far_rows = own_parts(repeats, own, first_weight, second_weight, [])
+    act, pre, row_grads, far_rows = own_parts(repeats, own, first_weight, second_weight)
     far_other = []
     for hop in range(repeats - 1):
         for turn in range(1, halves):
@@ -304,6 +364,7 @@
     returned = lax.all_to_all(
         row_grads.reshape(repeats * groups, capacity, model_width), ("rep", "grp"), 0, 0
     )
+    own, act, pre, first_weight, second_weight = stage([own, act, pre, first_weight, second_weight])
     grad_first, grad_second = rest_parts(
         halves, own, act, pre, near_other + far_other, first_weight, second_weight
     )

time: 90.9 us -> 89.8 us (0.988)
  waiting for transfers between devices: 17 us -> 12.1 us
  local copies, waits for them, and re-layouts: 2.21 us -> 5.98 us
  Pallas kernels: 19.3 us -> 17.9 us
  other arithmetic: 0.88 us -> 1.97 us
    ppermute x8, waiting for transfers between devices: 17 us -> 12.1 us  [on_device(): lax.ppermute(near[step], ('grp', 'dp'), across(turn, step))]
    unnamed x16 -> x20, local copies, waits for them, and re-layouts: 2.21 us -> 5.98 us
    pallas_call x1, Pallas kernels: 9.73 us -> 7.75 us  [rest_parts(): pl.pallas_call(functools.partial(rest_kernel, len(others)), out_shape=[ja...]
    reduce_sum x1, other arithmetic: 0.88 us -> 1.97 us  [on_device(): jnp.sum(returned.reshape(repeats, groups * capacity, model_width).astype(...]
    pallas_call x1 -> x2, Pallas kernels: 7.11 us -> 7.75 us  [the longest x1 6.94 us: own_parts(): pl.pallas_call(functools.partial(own_kernel, repeats), out_shape=[wide, w...]
  transfers between devices with their start and end apart: 10 -> 10, of which waited for: 3 -> 1; matrix products, arithmetic and copies ran while one was open for 0% -> 0% of each run, Pallas kernels for 11% -> 10%
where the time goes in v1:
time: 89.8 us; the launch traced here: 89.3 us
  blocking collectives  32.6 us (36%)
  starting transfers between devices  18 us (20%)
  Pallas kernels  17.9 us (20%)
  waiting for transfers between devices  12.1 us (13%)
  local copies, waits for them, and re-layouts  5.98 us (7%)
  other arithmetic  1.97 us (2%)
    all_to_all x1, blocking collectives, on_device(): own_rows = lax.all_to_all(outgoing, ('rep', 'grp'), 0, 0)  32.6 us
    ppermute x8, starting transfers between devices, on_device(): lax.ppermute(near[step], ('grp', 'dp'), across(turn, step))  12.3 us
    ppermute x8, waiting for transfers between devices, on_device(): lax.ppermute(near[step], ('grp', 'dp'), across(turn, step))  12.1 us
    pallas_call x1, Pallas kernels, rest_parts(): pl.pallas_call(functools.partial(rest_kernel, len(others)), out_shape=[ja...  7.75 us
    pallas_call x1, Pallas kernels, own_parts(): pl.pallas_call(functools.partial(own_kernel, repeats), out_shape=[wide, w...  6.94 us
    unnamed x20, local copies, waits for them, and re-layouts  5.98 us
    all_to_all x1, starting transfers between devices, on_device(): lax.all_to_all(row_grads.reshape(repeats * groups, capacity, model_width)...  4.48 us
    pallas_call x1, Pallas kernels, pack_blocks(): pl.pallas_call(functools.partial(pack_kernel, repeats, groups, capacity),...  2.42 us
  transfers between devices with their start and end apart: 10, of which 1 were waited for; matrix products, arithmetic and copies ran while one was open for 0% of the time, Pallas kernels for 10%

profile of v1, /device:TPU:1, one launch (start us, length us, event | category | flops | bytes accessed | tf_op | source)
XLA Modules:
  0.0 89.3 jit_solution(2641696633674986949)
XLA Ops:
  0.6 2.4 %pack_blocks.1 = (bf16[16,16,2048]{2,1,0:T(8,128)(2,1)}, bf16[16,2048]{1,0:T(8,128)(2,1)}, bf16[16,2048]{1,0:T(8,128)(2,1)}, bf16[16,2048]{1,0:T(8,128)(2,1)}, b...) custom-call(s32[128]{0:T(128)} %ids.1, ...), custom_call_target="tpu_custom_call" | custom-call | tf_op jit(solution)/shard_map/pack_blocks/pallas_call | solution.py:84
  3.0 32.6 %all_to_all.10 = bf16[16,16,2048]{2,1,0:T(8,128)(2,1)S(1)} all-to-all(bf16[16,16,2048]{2,1,0:T(8,128)(2,1)} %get-tuple-element.23), channel_id=1, replica_groups=mesh['rep'=2,'grp'=8,'dp'=2] {'rep','grp'}, dimensions={0} | all-to-all | bytes 2097152 | tf_op jit(solution)/shard_map/all_to_all | solution.py:351
  35.6 6.9 %own_parts.1 = (bf16[256,2048]{1,0:T(8,128)(2,1)S(1)}, bf16[256,2048]{1,0:T(8,128)(2,1)S(1)}, bf16[256,1024]{1,0:T(8,128)(2,1)S(1)}, bf16[1,128,2048]{2,1,0:T(8,128)(2,1)S(1)}) custom-call(bf16[256,2048]{1,0:T(8,128)(2,1)S(1)} %bitcast.15, bf16[1024,2048]{1,0:T(8,128)(2,1)} %bitcast.11, bf16[2048,1024]{1,0:T(8,128)(2,1)} %bitcast.13), custom_call_target="tpu_custom_call" | custom-call | flops 3221225472 | bytes 8388608 | tf_op jit(solution)/shard_map/own_parts/pallas_call | solution.py:194
  42.6 0.0 copy-start.2
  42.6 0.8 copy-done.2
  43.4 0.8 copy-done.3
  44.2 4.5 %all-to-all-start.1 = ((bf16[16,16,1024]{2,1,0:T(8,128)(2,1)}), bf16[16,16,1024]{2,1,0:T(8,128)(2,1)}, u32[]{:S(2)}, u32[]{:S(2)}) async-start(bf16[16,16,1024]{2,1,0:T(8,128)(2,1)} %bitcast.17), calls=%async_computation.1 | async-start | bytes 1048576 | tf_op jit(solution)/shard_map/all_to_all | solution.py:364
  48.6 1.2 %collective-permute-start.8 = (bf16[128,2048]{1,0:T(8,128)(2,1)}, bf16[128,2048]{1,0:T(8,128)(2,1)S(1)}, u32[]{:S(2)}, u32[]{:S(2)}) collective-permute-start(bf16[128,2048]{1,0:T(8,128)(2,1)} %bitcast.18), channel_id=1, source_target_pairs={{0,1},{1,0},{2,3},{3,2},{4,5},{5,4},{6,7},{7,6},{8,9},{9,8},{10,11... | collective-permute-start | bytes 1572872 | tf_op jit(solution)/shard_map/ppermute | solution.py:363
  49.9 0.2 collective-permute-start
  50.1 1.9 %collective-permute-start.1 = (bf16[16,2048]{1,0:T(8,128)(2,1)}, bf16[16,2048]{1,0:T(8,128)(2,1)S(1)}, u32[]{:S(2)}, u32[]{:S(2)}) collective-permute-start(bf16[16,2048]{1,0:T(8,128)(2,1)} %get-tuple-element.31), channel_id=1, source_target_pairs={{0,3},{1,2},{2,1},{3,0},{4,7},{5,6},{6,5},{7,4},{8,11},{9,10},{10,... | collective-permute-start | bytes 196616 | tf_op jit(solution)/shard_map/ppermute | solution.py:353
  52.0 1.5 %collective-permute-start.2 = (bf16[16,2048]{1,0:T(8,128)(2,1)S(1)}, bf16[16,2048]{1,0:T(8,128)(2,1)S(1)}, u32[]{:S(2)}, u32[]{:S(2)}) collective-permute-start(bf16[16,2048]{1,0:T(8,128)(2,1)S(1)} %copy-done.9), channel_id=1, source_target_pairs={{0,5},{1,4},{2,7},{3,6},{4,1},{5,0},{6,3},{7,2},{8,13},{9,12},{10,... | collective-permute-start | bytes 196616 | tf_op jit(solution)/shard_map/ppermute | solution.py:353
  53.5 0.8 collective-permute-start.3
  54.3 12.1 %collective-permute-done.refs_0_ = bf16[16,2048]{1,0:T(8,128)(2,1)S(1)} collective-permute-done((bf16[16,2048]{1,0:T(8,128)(2,1)}, bf16[16,2048]{1,0:T(8,128)(2,1)S(1)}, u32[]{:S(2)}, u32[]{:S(2)}) %collective-permute-start) | collective-permute-done | bytes 65568 | tf_op jit(solution)/shard_map/ppermute | solution.py:353
  66.3 2.2 %collective-permute-start.4 = (bf16[16,2048]{1,0:T(8,128)(2,1)S(1)}, bf16[16,2048]{1,0:T(8,128)(2,1)S(1)}, u32[]{:S(2)}, u32[]{:S(2)}) collective-permute-start(bf16[16,2048]{1,0:T(8,128)(2,1)S(1)} %copy-done.7), channel_id=1, source_target_pairs={{0,9},{1,8},{2,11},{3,10},{4,13},{5,12},{6,15},{7,14},{8,1},{9,0},... | collective-permute-start | bytes 196616 | tf_op jit(solution)/shard_map/ppermute | solution.py:353
  68.5 0.0 collective-permute-done.1.refs_1_
  68.5 2.1 %collective-permute-start.5 = (bf16[16,2048]{1,0:T(8,128)(2,1)S(1)}, bf16[16,2048]{1,0:T(8,128)(2,1)S(1)}, u32[]{:S(2)}, u32[]{:S(2)}) collective-permute-start(bf16[16,2048]{1,0:T(8,128)(2,1)S(1)} %copy-done.6), channel_id=1, source_target_pairs={{0,11},{1,10},{2,9},{3,8},{4,15},{5,14},{6,13},{7,12},{8,3},{9,2},... | collective-permute-start | bytes 196616 | tf_op jit(solution)/shard_map/ppermute | solution.py:353
  70.6 0.0 collective-permute-done.2.refs_2_
  70.6 3.2 %collective-permute-start.6 = (bf16[16,2048]{1,0:T(8,128)(2,1)S(1)}, bf16[16,2048]{1,0:T(8,128)(2,1)S(1)}, u32[]{:S(2)}, u32[]{:S(2)}) collective-permute-start(bf16[16,2048]{1,0:T(8,128)(2,1)S(1)} %copy-done.5), channel_id=1, source_target_pairs={{0,13},{1,12},{2,15},{3,14},{4,9},{5,8},{6,11},{7,10},{8,5},{9,4},... | collective-permute-start | bytes 196616 | tf_op jit(solution)/shard_map/ppermute | solution.py:353
  73.9 0.4 collective-permute-start.7
  74.3 2.2 %copy-done = bf16[1,1024,2048]{2,1,0:T(8,128)(2,1)S(1)} copy-done((bf16[1,1024,2048]{2,1,0:T(8,128)(2,1)S(1)}, bf16[1,1024,2048]{2,1,0:T(8,128)(2,1)}, u32[]{:S(2)}) %copy-start) | copy-done | bytes 4194328
  76.5 2.2 %copy-done.1 = bf16[1,2048,1024]{2,1,0:T(8,128)(2,1)S(1)} copy-done((bf16[1,2048,1024]{2,1,0:T(8,128)(2,1)S(1)}, bf16[1,2048,1024]{2,1,0:T(8,128)(2,1)}, u32[]{:S(2)}) %copy-start.1) | copy-done | bytes 4194328
  78.7 0.8 stage.1
  79.5 7.8 %rest_parts.1 = (f32[512,2048]{1,0:T(8,128)}, f32[1024,1024]{1,0:T(8,128)}) custom-call(bf16[256,2048]{1,0:T(8,128)(2,1)S(1)} %get-tuple-element.27.own_ref, bf16[256,2048]{1,0:T(8,128)(2,1)S(1)} %get-tuple-element.28.act_ref, bf16[256,2048]{1,0:T(8,128)(2,1)S(1)} %get-tuple-element.29.pre_ref, bf16[16,2048]{1,0:T(8,128)(2,1)S(1)} %collective-permute-done.refs_0_, ...), custom_call_target="tpu_custom_call" | custom-call | flops 4294967296 | bytes 8388608 | tf_op jit(solution)/shard_map/rest_parts/pallas_call | solution.py:304
  87.3 2.0 %convert_reduce_fusion = f32[128,1024]{1,0:T(8,128)} fusion(bf16[2,128,1024]{2,1,0:T(8,128)(2,1)} %bitcast.10), kind=kLoop, calls=%fused_computation | loop fusion | flops 393216 | bytes 1048576 | tf_op jit(solution)/shard_map/reduce_sum | solution.py:371
  (22 shorter events, 0.0 us)
Async XLA Ops:
  35.6 16.4 %copy-start.9 = (bf16[16,2048]{1,0:T(8,128)(2,1)S(1)}, bf16[16,2048]{1,0:T(8,128)(2,1)}, u32[]{:S(2)}) copy-start(bf16[16,2048]{1,0:T(8,128)(2,1)} %get-tuple-element.32) | copy-start | bytes 196612
  35.6 17.9 %copy-start.8 = (bf16[16,2048]{1,0:T(8,128)(2,1)S(1)}, bf16[16,2048]{1,0:T(8,128)(2,1)}, u32[]{:S(2)}) copy-start(bf16[16,2048]{1,0:T(8,128)(2,1)} %get-tuple-element.33) | copy-start | bytes 196612
  35.6 30.7 %copy-start.7 = (bf16[16,2048]{1,0:T(8,128)(2,1)S(1)}, bf16[16,2048]{1,0:T(8,128)(2,1)}, u32[]{:S(2)}) copy-start(bf16[16,2048]{1,0:T(8,128)(2,1)} %get-tuple-element.34) | copy-start | bytes 196612
  35.6 32.9 %copy-start.6 = (bf16[16,2048]{1,0:T(8,128)(2,1)S(1)}, bf16[16,2048]{1,0:T(8,128)(2,1)}, u32[]{:S(2)}) copy-start(bf16[16,2048]{1,0:T(8,128)(2,1)} %get-tuple-element.35) | copy-start | bytes 196612
  35.6 35.0 %copy-start.5 = (bf16[16,2048]{1,0:T(8,128)(2,1)S(1)}, bf16[16,2048]{1,0:T(8,128)(2,1)}, u32[]{:S(2)}) copy-start(bf16[16,2048]{1,0:T(8,128)(2,1)} %get-tuple-element.36) | copy-start | bytes 196612
  35.6 38.2 %copy-start.4 = (bf16[16,2048]{1,0:T(8,128)(2,1)S(1)}, bf16[16,2048]{1,0:T(8,128)(2,1)}, u32[]{:S(2)}) copy-start(bf16[16,2048]{1,0:T(8,128)(2,1)} %get-tuple-element.37) | copy-start | bytes 196612
  42.6 0.8 copy-start.2
  43.4 0.8 copy-start.3
  44.2 43.1 %all-to-all-start.1 = ((bf16[16,16,1024]{2,1,0:T(8,128)(2,1)}), bf16[16,16,1024]{2,1,0:T(8,128)(2,1)}, u32[]{:S(2)}, u32[]{:S(2)}) async-start(bf16[16,16,1024]{2,1,0:T(8,128)(2,1)} %bitcast.17), calls=%async_computation.1 | async-start | bytes 1048576 | tf_op jit(solution)/shard_map/all_to_all | solution.py:364
  48.6 30.9 %collective-permute-start.8 = (bf16[128,2048]{1,0:T(8,128)(2,1)}, bf16[128,2048]{1,0:T(8,128)(2,1)S(1)}, u32[]{:S(2)}, u32[]{:S(2)}) collective-permute-start(bf16[128,2048]{1,0:T(8,128)(2,1)} %bitcast.18), channel_id=1, source_target_pairs={{0,1},{1,0},{2,3},{3,2},{4,5},{5,4},{6,7},{7,6},{8,9},{9,8},{10,11... | collective-permute-start | bytes 1572872 | tf_op jit(solution)/shard_map/ppermute | solution.py:363
  49.9 16.4 %collective-permute-start = (bf16[16,2048]{1,0:T(8,128)(2,1)}, bf16[16,2048]{1,0:T(8,128)(2,1)S(1)}, u32[]{:S(2)}, u32[]{:S(2)}) collective-permute-start(bf16[16,2048]{1,0:T(8,128)(2,1)} %get-tuple-element.30), channel_id=1, source_target_pairs={{0,1},{1,0},{2,3},{3,2},{4,5},{5,4},{6,7},{7,6},{8,9},{9,8},{10,11... | collective-permute-start | bytes 196616 | tf_op jit(solution)/shard_map/ppermute | solution.py:353
  50.1 18.4 %collective-permute-start.1 = (bf16[16,2048]{1,0:T(8,128)(2,1)}, bf16[16,2048]{1,0:T(8,128)(2,1)S(1)}, u32[]{:S(2)}, u32[]{:S(2)}) collective-permute-start(bf16[16,2048]{1,0:T(8,128)(2,1)} %get-tuple-element.31), channel_id=1, source_target_pairs={{0,3},{1,2},{2,1},{3,0},{4,7},{5,6},{6,5},{7,4},{8,11},{9,10},{10,... | collective-permute-start | bytes 196616 | tf_op jit(solution)/shard_map/ppermute | solution.py:353
  52.0 18.6 %collective-permute-start.2 = (bf16[16,2048]{1,0:T(8,128)(2,1)S(1)}, bf16[16,2048]{1,0:T(8,128)(2,1)S(1)}, u32[]{:S(2)}, u32[]{:S(2)}) collective-permute-start(bf16[16,2048]{1,0:T(8,128)(2,1)S(1)} %copy-done.9), channel_id=1, source_target_pairs={{0,5},{1,4},{2,7},{3,6},{4,1},{5,0},{6,3},{7,2},{8,13},{9,12},{10,... | collective-permute-start | bytes 196616 | tf_op jit(solution)/shard_map/ppermute | solution.py:353
  53.5 20.4 %collective-permute-start.3 = (bf16[16,2048]{1,0:T(8,128)(2,1)S(1)}, bf16[16,2048]{1,0:T(8,128)(2,1)S(1)}, u32[]{:S(2)}, u32[]{:S(2)}) collective-permute-start(bf16[16,2048]{1,0:T(8,128)(2,1)S(1)} %copy-done.8), channel_id=1, source_target_pairs={{0,7},{1,6},{2,5},{3,4},{4,3},{5,2},{6,1},{7,0},{8,15},{9,14},{10,... | collective-permute-start | bytes 196616 | tf_op jit(solution)/shard_map/ppermute | solution.py:353
  66.3 13.2 %collective-permute-start.4 = (bf16[16,2048]{1,0:T(8,128)(2,1)S(1)}, bf16[16,2048]{1,0:T(8,128)(2,1)S(1)}, u32[]{:S(2)}, u32[]{:S(2)}) collective-permute-start(bf16[16,2048]{1,0:T(8,128)(2,1)S(1)} %copy-done.7), channel_id=1, source_target_pairs={{0,9},{1,8},{2,11},{3,10},{4,13},{5,12},{6,15},{7,14},{8,1},{9,0},... | collective-permute-start | bytes 196616 | tf_op jit(solution)/shard_map/ppermute | solution.py:353
  68.5 11.0 %collective-permute-start.5 = (bf16[16,2048]{1,0:T(8,128)(2,1)S(1)}, bf16[16,2048]{1,0:T(8,128)(2,1)S(1)}, u32[]{:S(2)}, u32[]{:S(2)}) collective-permute-start(bf16[16,2048]{1,0:T(8,128)(2,1)S(1)} %copy-done.6), channel_id=1, source_target_pairs={{0,11},{1,10},{2,9},{3,8},{4,15},{5,14},{6,13},{7,12},{8,3},{9,2},... | collective-permute-start | bytes 196616 | tf_op jit(solution)/shard_map/ppermute | solution.py:353
  70.6 8.9 %collective-permute-start.6 = (bf16[16,2048]{1,0:T(8,128)(2,1)S(1)}, bf16[16,2048]{1,0:T(8,128)(2,1)S(1)}, u32[]{:S(2)}, u32[]{:S(2)}) collective-permute-start(bf16[16,2048]{1,0:T(8,128)(2,1)S(1)} %copy-done.5), channel_id=1, source_target_pairs={{0,13},{1,12},{2,15},{3,14},{4,9},{5,8},{6,11},{7,10},{8,5},{9,4},... | collective-permute-start | bytes 196616 | tf_op jit(solution)/shard_map/ppermute | solution.py:353
  73.9 5.7 %collective-permute-start.7 = (bf16[16,2048]{1,0:T(8,128)(2,1)S(1)}, bf16[16,2048]{1,0:T(8,128)(2,1)S(1)}, u32[]{:S(2)}, u32[]{:S(2)}) collective-permute-start(bf16[16,2048]{1,0:T(8,128)(2,1)S(1)} %copy-done.4), channel_id=1, source_target_pairs={{0,15},{1,14},{2,13},{3,12},{4,11},{5,10},{6,9},{7,8},{8,7},{9,6},... | collective-permute-start | bytes 196616 | tf_op jit(solution)/shard_map/ppermute | solution.py:353
  74.3 2.2 %copy-start = (bf16[1,1024,2048]{2,1,0:T(8,128)(2,1)S(1)}, bf16[1,1024,2048]{2,1,0:T(8,128)(2,1)}, u32[]{:S(2)}) copy-start(bf16[1,1024,2048]{2,1,0:T(8,128)(2,1)} %param.12) | copy-start | bytes 12582916
  76.5 2.2 %copy-start.1 = (bf16[1,2048,1024]{2,1,0:T(8,128)(2,1)S(1)}, bf16[1,2048,1024]{2,1,0:T(8,128)(2,1)}, u32[]{:S(2)}) copy-start(bf16[1,2048,1024]{2,1,0:T(8,128)(2,1)} %param.13) | copy-start | bytes 12582916

commit v2 on v1

--- a/solution.py
+++ b/solution.py
@@ -11,8 +11,9 @@
 
 grad_scale = 0.0625
 lanes = 128
-own_tile = 256
-rest_tile = 512
+own_tile = 512
+rest_tile = 1024
+last_tile = 512
 kernel_grant = 48 << 20
 load_depth = 4
 stage_grant = 1 << 20
@@ -143,21 +144,24 @@
     return value.astype(jnp.bfloat16), (hidden_cot * slope).astype(jnp.bfloat16)
 
 
-def own_kernel(repeats, rows_ref, first_hbm, second_hbm, *refs):
-    act_hbm, pre_hbm, grad_ref, far_ref = refs[:4]
-    act_ref, pre_ref, total_ref, out_sems, first_ref, second_ref, sems = refs[4:]
+def own_kernel(repeats, halves, rows_ref, first_hbm, second_hbm, *refs):
+    act_out, pre_ref, x_ref, scaled_ref, grad_ref, far_ref = refs[:6]
+    act_ref, total_ref, first_ref, second_ref, sems = refs[6:]
     row_count = rows_ref.shape[0]
     model_width, hidden_width = first_ref.shape
     copies = weight_copies(own_tile, first_hbm, second_hbm, first_ref, second_ref, sems)
     per_repeat = row_count // repeats
     own_repeat = lax.axis_index("rep")
+    half = lax.axis_index("dp")
     for hop in range(1, repeats):
         source = lax.rem(own_repeat + hop, repeats)
         start = pl.multiple_of(source * per_repeat, per_repeat)
         far_ref[hop - 1] = rows_ref[pl.ds(start, per_repeat), :]
+    first_rows = model_width // halves
+    x_ref[...] = rows_ref[:, pl.ds(pl.multiple_of(half * first_rows, first_rows), first_rows)]
+    scaled_ref[...] = rows_ref[:, model_width:]
     x_rows = rows_ref[:, :model_width]
     scaled_cot = rows_ref[:, model_width:]
-    stores = []
     last = hidden_width // own_tile - 1
     for index in range(last + 1):
         columns = slice(index * own_tile, (index + 1) * own_tile)
@@ -165,6 +169,10 @@
         act, pre = hidden_chunk(x_rows, scaled_cot, first_ref[:, columns], second_ref[columns, :])
         act_ref[:, columns] = act
         pre_ref[:, columns] = pre
+        if index == last:
+            second_rows = hidden_width // halves
+            begin = pl.multiple_of(half * second_rows, second_rows)
+            act_out[...] = act_ref[:, pl.ds(begin, second_rows)]
         part = contract(pre, first_ref[:, columns], 1, 1)
         if index == 0:
             total_ref[...] = part
@@ -172,40 +180,30 @@
             total_ref[...] += part
         else:
             grad_ref[...] = (total_ref[...] + part).astype(jnp.bfloat16)
-        stores.append(
-            (
-                pltpu.make_async_copy(
-                    act_ref.at[:, columns], act_hbm.at[:, columns], out_sems.at[2 * index]
-                ),
-                pltpu.make_async_copy(
-                    pre_ref.at[:, columns], pre_hbm.at[:, columns], out_sems.at[2 * index + 1]
-                ),
-            )
-        )
-        start_pair(stores[-1])
-    for pair in stores:
-        wait_pair(pair)
-
-
-def own_parts(repeats, rows, first_weight, second_weight):
+
+
+def own_parts(repeats, halves, rows, first_weight, second_weight):
     row_count, width = rows.shape
     model_width, hidden_width = first_weight.shape
-    wide = jax.ShapeDtypeStruct((row_count, hidden_width), jnp.bfloat16)
+
+    def shaped(*shape):
+        return jax.ShapeDtypeStruct(shape, jnp.bfloat16)
+
     return pl.pallas_call(
-        functools.partial(own_kernel, repeats),
+        functools.partial(own_kernel, repeats, halves),
         out_shape=[
-            wide,
-            wide,
-            jax.ShapeDtypeStruct((row_count, model_width), jnp.bfloat16),
-            jax.ShapeDtypeStruct((repeats - 1, row_count // repeats, width), jnp.bfloat16),
+            shaped(row_count, hidden_width // halves),
+            shaped(row_count, hidden_width),
+            shaped(row_count, model_width // halves),
+            shaped(row_count, model_width),
+            shaped(row_count, model_width),
+            shaped(repeats - 1, row_count // repeats, width),
         ],
         in_specs=[vmem_spec, any_spec, any_spec],
-        out_specs=[hbm_spec, hbm_spec, vmem_spec, vmem_spec],
+        out_specs=[vmem_spec] * 6,
         scratch_shapes=[
-            pltpu.VMEM(wide.shape, wide.dtype),
-            pltpu.VMEM(wide.shape, wide.dtype),
+            pltpu.VMEM((row_count, hidden_width), jnp.bfloat16),
             pltpu.VMEM((row_count, model_width), jnp.float32),
-            pltpu.SemaphoreType.DMA((2 * hidden_width // own_tile,)),
             *weight_scratch(first_weight, second_weight, own_tile),
         ],
         compiler_params=pltpu.CompilerParams(vmem_limit_bytes=kernel_grant),
@@ -240,11 +238,12 @@
     )(*arrays)
 
 
-def rest_kernel(other_count, own_ref, act_ref, pre_ref, *refs):
+def rest_kernel(other_count, act_ref, pre_ref, x_ref, scaled_ref, *refs):
     other_refs = refs[:other_count]
     first_ref, second_ref, first_out, second_out = refs[other_count : other_count + 4]
-    other, other_act, left, first_buf, second_buf, sems = refs[other_count + 4 :]
-    own_count = own_ref.shape[0]
+    scratch = refs[other_count + 4 :]
+    other, other_act, all_act, all_pre, scaled, left, first_buf, second_buf, sems = scratch
+    own_count = act_ref.shape[0]
     model_width, _ = first_ref.shape
     first_tiles, first_rows, first_tile = first_buf.shape
     second_tiles, second_tile, _ = second_buf.shape
@@ -254,8 +253,11 @@
         other[place : place + ref.shape[0], :] = ref[...]
         place += ref.shape[0]
     x_begin = pl.multiple_of(half * first_rows, first_rows)
-    left[:, :own_count] = own_ref[:, pl.ds(x_begin, first_rows)].T
+    left[:, :own_count] = x_ref[...].T
     left[:, own_count:] = other[:, pl.ds(x_begin, first_rows)].T
+    scaled[:own_count, :] = scaled_ref[...]
+    scaled[own_count:, :] = other[:, model_width:]
+    all_act[:own_count, :] = act_ref[...]
     copies = []
     for tile in range(first_tiles):
         columns = slice(tile * first_tile, (tile + 1) * first_tile)
@@ -266,22 +268,21 @@
             second_ref[columns, :],
         )
         other_act[:, columns] = act
-        total = contract(left[:, :own_count], pre_ref[:, columns], 1, 0)
-        total += contract(left[:, own_count:], pre, 1, 0)
-        first_buf[tile] = total * grad_scale
+        all_pre[:own_count, :] = pre_ref[:, columns]
+        all_pre[own_count:, :] = pre
+        first_buf[tile] = contract(left[...], all_pre[...], 1, 0) * grad_scale
         if copies:
             copies[-1].start()
         copies.append(
             pltpu.make_async_copy(first_buf.at[tile], first_out.at[:, columns], sems.at[tile])
         )
+    second_rows = second_tiles * second_tile
+    begin = pl.multiple_of(half * second_rows, second_rows)
+    all_act[own_count:, :] = other_act[:, pl.ds(begin, second_rows)]
     for tile in range(second_tiles):
-        begin = half * (second_tiles * second_tile) + tile * second_tile
-        columns = pl.ds(pl.multiple_of(begin, second_tile), second_tile)
-        total = contract(act_ref[:, columns].T, own_ref[:, model_width:], 1, 0)
-        total += contract(other_act[:, columns].T, other[:, model_width:], 1, 0)
-        second_buf[tile] = total * grad_scale
+        rows = slice(tile * second_tile, (tile + 1) * second_tile)
+        second_buf[tile] = contract(all_act[:, rows].T, scaled[...], 1, 0) * grad_scale
         copies[-1].start()
-        rows = slice(tile * second_tile, (tile + 1) * second_tile)
         copies.append(
             pltpu.make_async_copy(
                 second_buf.at[tile], second_out.at[rows, :], sems.at[first_tiles + tile]
@@ -292,13 +293,14 @@
         copy.wait()
 
 
-def rest_parts(halves, own, act, pre, others, first_weight, second_weight):
-    own_count, width = own.shape
+def rest_parts(own, others, first_weight, second_weight):
+    own_count, second_rows = own[0].shape
+    first_rows = own[2].shape[1]
+    width = others[0].shape[1]
     model_width, hidden_width = first_weight.shape
     other_rows = sum(part.shape[0] for part in others)
-    first_rows, second_rows = model_width // halves, hidden_width // halves
     first_tiles = hidden_width // rest_tile
-    second_tiles = second_rows // rest_tile
+    second_tiles = second_rows // last_tile
     row_count = own_count + other_rows
     flops = 4 * (row_count * first_rows + other_rows * model_width) * hidden_width
     return pl.pallas_call(
@@ -307,24 +309,27 @@
             jax.ShapeDtypeStruct((first_rows, hidden_width), jnp.float32),
             jax.ShapeDtypeStruct((second_rows, model_width), jnp.float32),
         ],
-        in_specs=[vmem_spec] * (5 + len(others)),
+        in_specs=[vmem_spec] * (6 + len(others)),
         out_specs=[hbm_spec, hbm_spec],
         scratch_shapes=[
             pltpu.VMEM((other_rows, width), jnp.bfloat16),
             pltpu.VMEM((other_rows, hidden_width), jnp.bfloat16),
+            pltpu.VMEM((row_count, second_rows), jnp.bfloat16),
+            pltpu.VMEM((row_count, rest_tile), jnp.bfloat16),
+            pltpu.VMEM((row_count, model_width), jnp.bfloat16),
             pltpu.VMEM((first_rows, row_count), jnp.bfloat16),
             pltpu.VMEM((first_tiles, first_rows, rest_tile), jnp.float32),
-            pltpu.VMEM((second_tiles, rest_tile, model_width), jnp.float32),
+            pltpu.VMEM((second_tiles, last_tile, model_width), jnp.float32),
             pltpu.SemaphoreType.DMA((first_tiles + second_tiles,)),
         ],
         compiler_params=pltpu.CompilerParams(
-            vmem_limit_bytes=min(60 << 20, (16 << 20) + row_count * (32 << 10))
+            vmem_limit_bytes=min(60 << 20, (20 << 20) + row_count * (24 << 10))
         ),
         cost_estimate=pl.CostEstimate(
             flops=flops, bytes_accessed=8 * first_rows * hidden_width, transcendentals=0
         ),
         name="rest_parts",
-    )(own, act, pre, *others, first_weight, second_weight)
+    )(*own, *others, first_weight, second_weight)
 
 
 def on_device(inputs, cotangent, task_ids, group_counts, task_gate, w_in, w_out):
@@ -355,7 +360,7 @@
         for step in range(groups)
     ]
     own = own_rows.reshape(repeats * groups * capacity, width)
-    act, pre, row_grads, far_rows = own_parts(repeats, own, first_weight, second_weight)
+    *own_kept, row_grads, far_rows = own_parts(repeats, halves, own, first_weight, second_weight)
     far_other = []
     for hop in range(repeats - 1):
         for turn in range(1, halves):
@@ -364,9 +369,9 @@
     returned = lax.all_to_all(
         row_grads.reshape(repeats * groups, capacity, model_width), ("rep", "grp"), 0, 0
     )
-    own, act, pre, first_weight, second_weight = stage([own, act, pre, first_weight, second_weight])
+    *own_kept, first_weight, second_weight = stage([*own_kept, first_weight, second_weight])
     grad_first, grad_second = rest_parts(
-        halves, own, act, pre, near_other + far_other, first_weight, second_weight
+        own_kept, near_other + far_other, first_weight, second_weight
     )
     input_home = jnp.sum(
         returned.reshape(repeats, groups * capacity, model_width).astype(jnp.float32), axis=0

time: 89.8 us -> 86.2 us (0.960)
  local copies, waits for them, and re-layouts: 5.98 us -> 4.38 us
  other arithmetic: 1.97 us -> 0.88 us
    unnamed x20 -> x8, local copies, waits for them, and re-layouts: 5.98 us -> 4.38 us
    reduce_sum x1, other arithmetic: 1.97 us -> 0.88 us  [on_device(): jnp.sum(returned.reshape(repeats, groups * capacity, model_width).astype(...]
  transfers between devices with their start and end apart: 10 -> 10, of which waited for: 1 -> 1; matrix products, arithmetic and copies ran while one was open for 0% -> 0% of each run, Pallas kernels for 10% -> 9%
where the time goes in v2:
time: 86.2 us; the launch traced here: 85.8 us
  blocking collectives  32.6 us (38%)
  starting transfers between devices  18 us (21%)
  Pallas kernels  17.3 us (20%)
  waiting for transfers between devices  11.9 us (14%)
  local copies, waits for them, and re-layouts  4.38 us (5%)
  other arithmetic  0.88 us (1%)
    all_to_all x1, blocking collectives, on_device(): own_rows = lax.all_to_all(outgoing, ('rep', 'grp'), 0, 0)  32.6 us
    ppermute x8, starting transfers between devices, on_device(): lax.ppermute(near[step], ('grp', 'dp'), across(turn, step))  12.3 us
    ppermute x8, waiting for transfers between devices, on_device(): lax.ppermute(near[step], ('grp', 'dp'), across(turn, step))  11.9 us
    pallas_call x1, Pallas kernels, rest_parts(): pl.pallas_call(functools.partial(rest_kernel, len(others)), out_shape=[ja...  7.34 us
    pallas_call x1, Pallas kernels, own_parts(): pl.pallas_call(functools.partial(own_kernel, repeats, halves), out_shape=...  6.79 us
    all_to_all x1, starting transfers between devices, on_device(): lax.all_to_all(row_grads.reshape(repeats * groups, capacity, model_width)...  4.49 us
    unnamed x8, local copies, waits for them, and re-layouts  4.38 us
    pallas_call x1, Pallas kernels, pack_blocks(): pl.pallas_call(functools.partial(pack_kernel, repeats, groups, capacity),...  2.42 us
  transfers between devices with their start and end apart: 10, of which 1 were waited for; matrix products, arithmetic and copies ran while one was open for 0% of the time, Pallas kernels for 9%

profile of v2, /device:TPU:1, one launch (start us, length us, event | category | flops | bytes accessed | tf_op | source)
XLA Modules:
  0.0 85.8 jit_solution(485150566431232235)
XLA Ops:
  0.6 2.4 %pack_blocks.1 = (bf16[16,16,2048]{2,1,0:T(8,128)(2,1)}, bf16[16,2048]{1,0:T(8,128)(2,1)}, bf16[16,2048]{1,0:T(8,128)(2,1)}, bf16[16,2048]{1,0:T(8,128)(2,1)}, b...) custom-call(s32[128]{0:T(128)} %ids.1, ...), custom_call_target="tpu_custom_call" | custom-call | tf_op jit(solution)/shard_map/pack_blocks/pallas_call | solution.py:85
  3.0 32.6 %all_to_all.10 = bf16[16,16,2048]{2,1,0:T(8,128)(2,1)S(1)} all-to-all(bf16[16,16,2048]{2,1,0:T(8,128)(2,1)} %get-tuple-element.26), channel_id=1, replica_groups=mesh['rep'=2,'grp'=8,'dp'=2] {'rep','grp'}, dimensions={0} | all-to-all | bytes 2097152 | tf_op jit(solution)/shard_map/all_to_all | solution.py:356
  35.6 6.8 %own_parts.1 = (bf16[256,1024]{1,0:T(8,128)(2,1)S(1)}, bf16[256,2048]{1,0:T(8,128)(2,1)S(1)}, bf16[256,512]{1,0:T(8,128)(2,1)S(1)}, bf16[256,1024]{1,0:T(8,128)(...) custom-call(bf16[256,2048]{1,0:T(8,128)(2,1)S(1)} %bitcast.15, bf16[1024,2048]{1,0:T(8,128)(2,1)} %bitcast.11, ...), custom_call_target="tpu_custom_call" | custom-call | flops 3221225472 | bytes 8388608 | tf_op jit(solution)/shard_map/own_parts/pallas_call | solution.py:192
  42.4 4.5 %all-to-all-start.1 = ((bf16[16,16,1024]{2,1,0:T(8,128)(2,1)}), bf16[16,16,1024]{2,1,0:T(8,128)(2,1)S(1)}, u32[]{:S(2)}, u32[]{:S(2)}) async-start(bf16[16,16,1024]{2,1,0:T(8,128)(2,1)} %bitcast.3), calls=%async_computation.1 | async-start | bytes 1048576 | tf_op jit(solution)/shard_map/all_to_all | solution.py:369
  46.9 1.3 %collective-permute-start.8 = (bf16[128,2048]{1,0:T(8,128)(2,1)S(1)}, bf16[128,2048]{1,0:T(8,128)(2,1)S(1)}, u32[]{:S(2)}, u32[]{:S(2)}) collective-permute-start(bf16[128,2048]{1,0:T(8,128)(2,1)S(1)} %bitcast.16), channel_id=1, source_target_pairs={{0,1},{1,0},{2,3},{3,2},{4,5},{5,4},{6,7},{7,6},{8,9},{9,8},{10,11... | collective-permute-start | bytes 1572872 | tf_op jit(solution)/shard_map/ppermute | solution.py:368
  48.2 0.2 collective-permute-start
  48.4 1.9 %collective-permute-start.1 = (bf16[16,2048]{1,0:T(8,128)(2,1)}, bf16[16,2048]{1,0:T(8,128)(2,1)S(1)}, u32[]{:S(2)}, u32[]{:S(2)}) collective-permute-start(bf16[16,2048]{1,0:T(8,128)(2,1)} %get-tuple-element.37), channel_id=1, source_target_pairs={{0,3},{1,2},{2,1},{3,0},{4,7},{5,6},{6,5},{7,4},{8,11},{9,10},{10,... | collective-permute-start | bytes 196616 | tf_op jit(solution)/shard_map/ppermute | solution.py:358
  50.2 1.5 %collective-permute-start.2 = (bf16[16,2048]{1,0:T(8,128)(2,1)}, bf16[16,2048]{1,0:T(8,128)(2,1)S(1)}, u32[]{:S(2)}, u32[]{:S(2)}) collective-permute-start(bf16[16,2048]{1,0:T(8,128)(2,1)} %get-tuple-element.38), channel_id=1, source_target_pairs={{0,5},{1,4},{2,7},{3,6},{4,1},{5,0},{6,3},{7,2},{8,13},{9,12},{10,... | collective-permute-start | bytes 196616 | tf_op jit(solution)/shard_map/ppermute | solution.py:358
  51.7 0.8 collective-permute-start.3
  52.5 11.9 %collective-permute-done.refs_0_ = bf16[16,2048]{1,0:T(8,128)(2,1)S(1)} collective-permute-done((bf16[16,2048]{1,0:T(8,128)(2,1)}, bf16[16,2048]{1,0:T(8,128)(2,1)S(1)}, u32[]{:S(2)}, u32[]{:S(2)}) %collective-permute-start) | collective-permute-done | bytes 65568 | tf_op jit(solution)/shard_map/ppermute | solution.py:358
  64.4 2.1 %collective-permute-start.4 = (bf16[16,2048]{1,0:T(8,128)(2,1)}, bf16[16,2048]{1,0:T(8,128)(2,1)S(1)}, u32[]{:S(2)}, u32[]{:S(2)}) collective-permute-start(bf16[16,2048]{1,0:T(8,128)(2,1)} %get-tuple-element.40), channel_id=1, source_target_pairs={{0,9},{1,8},{2,11},{3,10},{4,13},{5,12},{6,15},{7,14},{8,1},{9,0},... | collective-permute-start | bytes 196616 | tf_op jit(solution)/shard_map/ppermute | solution.py:358
  66.5 2.1 %collective-permute-start.5 = (bf16[16,2048]{1,0:T(8,128)(2,1)}, bf16[16,2048]{1,0:T(8,128)(2,1)S(1)}, u32[]{:S(2)}, u32[]{:S(2)}) collective-permute-start(bf16[16,2048]{1,0:T(8,128)(2,1)} %get-tuple-element.41), channel_id=1, source_target_pairs={{0,11},{1,10},{2,9},{3,8},{4,15},{5,14},{6,13},{7,12},{8,3},{9,2},... | collective-permute-start | bytes 196616 | tf_op jit(solution)/shard_map/ppermute | solution.py:358
  68.6 0.0 collective-permute-done.2.refs_2_
  68.6 3.3 %collective-permute-start.6 = (bf16[16,2048]{1,0:T(8,128)(2,1)S(1)}, bf16[16,2048]{1,0:T(8,128)(2,1)S(1)}, u32[]{:S(2)}, u32[]{:S(2)}) collective-permute-start(bf16[16,2048]{1,0:T(8,128)(2,1)S(1)} %copy-done.3), channel_id=1, source_target_pairs={{0,13},{1,12},{2,15},{3,14},{4,9},{5,8},{6,11},{7,10},{8,5},{9,4},... | collective-permute-start | bytes 196616 | tf_op jit(solution)/shard_map/ppermute | solution.py:358
  71.9 0.0 collective-permute-done.3.refs_3_
  71.9 0.4 collective-permute-start.7
  72.3 2.2 %copy-done = bf16[1,1024,2048]{2,1,0:T(8,128)(2,1)S(1)} copy-done((bf16[1,1024,2048]{2,1,0:T(8,128)(2,1)S(1)}, bf16[1,1024,2048]{2,1,0:T(8,128)(2,1)}, u32[]{:S(2)}) %copy-start) | copy-done | bytes 4194328
  74.5 2.2 %copy-done.1 = bf16[1,2048,1024]{2,1,0:T(8,128)(2,1)S(1)} copy-done((bf16[1,2048,1024]{2,1,0:T(8,128)(2,1)S(1)}, bf16[1,2048,1024]{2,1,0:T(8,128)(2,1)}, u32[]{:S(2)}) %copy-start.1) | copy-done | bytes 4194328
  76.7 0.8 stage.1
  77.5 0.0 collective-permute-done.5.refs_5_
  77.5 0.0 collective-permute-done.6.refs_6_
  77.5 0.0 collective-permute-done.8.refs_8_
  77.5 7.3 %rest_parts.1 = (f32[512,2048]{1,0:T(8,128)}, f32[1024,1024]{1,0:T(8,128)}) custom-call(bf16[256,1024]{1,0:T(8,128)(2,1)S(1)} %get-tuple-element.32.act_ref, bf16[256,2048]{1,0:T(8,128)(2,1)S(1)} %get-tuple-element.33.pre_ref, bf16[256,512]{1,0:T(8,128)(2,1)S(1)} %get-tuple-element.34.x_ref, bf16[256,1024]{1,0:T(8,128)(2,1)S(1)} %get-tuple-element.35.scaled_ref, ...), custom_call_target="tpu_custom_call" | custom-call | flops 4294967296 | bytes 8388608 | tf_op jit(solution)/shard_map/rest_parts/pallas_call | solution.py:306
  84.9 0.9 %convert_reduce_fusion = f32[128,1024]{1,0:T(8,128)} fusion(bf16[2,128,1024]{2,1,0:T(8,128)(2,1)S(1)} %bitcast.17), kind=kLoop, calls=%fused_computation | loop fusion | flops 393216 | bytes 1048576 | tf_op jit(solution)/shard_map/reduce_sum | solution.py:376
  (10 shorter events, 0.0 us)
Async XLA Ops:
  35.6 33.0 %copy-start.3 = (bf16[16,2048]{1,0:T(8,128)(2,1)S(1)}, bf16[16,2048]{1,0:T(8,128)(2,1)}, u32[]{:S(2)}) copy-start(bf16[16,2048]{1,0:T(8,128)(2,1)} %get-tuple-element.42) | copy-start | bytes 196612
  35.6 36.3 %copy-start.2 = (bf16[16,2048]{1,0:T(8,128)(2,1)S(1)}, bf16[16,2048]{1,0:T(8,128)(2,1)}, u32[]{:S(2)}) copy-start(bf16[16,2048]{1,0:T(8,128)(2,1)} %get-tuple-element.43) | copy-start | bytes 196612
  42.4 42.5 %all-to-all-start.1 = ((bf16[16,16,1024]{2,1,0:T(8,128)(2,1)}), bf16[16,16,1024]{2,1,0:T(8,128)(2,1)S(1)}, u32[]{:S(2)}, u32[]{:S(2)}) async-start(bf16[16,16,1024]{2,1,0:T(8,128)(2,1)} %bitcast.3), calls=%async_computation.1 | async-start | bytes 1048576 | tf_op jit(solution)/shard_map/all_to_all | solution.py:369
  46.9 30.6 %collective-permute-start.8 = (bf16[128,2048]{1,0:T(8,128)(2,1)S(1)}, bf16[128,2048]{1,0:T(8,128)(2,1)S(1)}, u32[]{:S(2)}, u32[]{:S(2)}) collective-permute-start(bf16[128,2048]{1,0:T(8,128)(2,1)S(1)} %bitcast.16), channel_id=1, source_target_pairs={{0,1},{1,0},{2,3},{3,2},{4,5},{5,4},{6,7},{7,6},{8,9},{9,8},{10,11... | collective-permute-start | bytes 1572872 | tf_op jit(solution)/shard_map/ppermute | solution.py:368
  48.2 16.3 %collective-permute-start = (bf16[16,2048]{1,0:T(8,128)(2,1)}, bf16[16,2048]{1,0:T(8,128)(2,1)S(1)}, u32[]{:S(2)}, u32[]{:S(2)}) collective-permute-start(bf16[16,2048]{1,0:T(8,128)(2,1)} %get-tuple-element.36), channel_id=1, source_target_pairs={{0,1},{1,0},{2,3},{3,2},{4,5},{5,4},{6,7},{7,6},{8,9},{9,8},{10,11... | collective-permute-start | bytes 196616 | tf_op jit(solution)/shard_map/ppermute | solution.py:358
  48.4 18.2 %collective-permute-start.1 = (bf16[16,2048]{1,0:T(8,128)(2,1)}, bf16[16,2048]{1,0:T(8,128)(2,1)S(1)}, u32[]{:S(2)}, u32[]{:S(2)}) collective-permute-start(bf16[16,2048]{1,0:T(8,128)(2,1)} %get-tuple-element.37), channel_id=1, source_target_pairs={{0,3},{1,2},{2,1},{3,0},{4,7},{5,6},{6,5},{7,4},{8,11},{9,10},{10,... | collective-permute-start | bytes 196616 | tf_op jit(solution)/shard_map/ppermute | solution.py:358
  50.2 18.4 %collective-permute-start.2 = (bf16[16,2048]{1,0:T(8,128)(2,1)}, bf16[16,2048]{1,0:T(8,128)(2,1)S(1)}, u32[]{:S(2)}, u32[]{:S(2)}) collective-permute-start(bf16[16,2048]{1,0:T(8,128)(2,1)} %get-tuple-element.38), channel_id=1, source_target_pairs={{0,5},{1,4},{2,7},{3,6},{4,1},{5,0},{6,3},{7,2},{8,13},{9,12},{10,... | collective-permute-start | bytes 196616 | tf_op jit(solution)/shard_map/ppermute | solution.py:358
  51.7 20.2 %collective-permute-start.3 = (bf16[16,2048]{1,0:T(8,128)(2,1)}, bf16[16,2048]{1,0:T(8,128)(2,1)S(1)}, u32[]{:S(2)}, u32[]{:S(2)}) collective-permute-start(bf16[16,2048]{1,0:T(8,128)(2,1)} %get-tuple-element.39), channel_id=1, source_target_pairs={{0,7},{1,6},{2,5},{3,4},{4,3},{5,2},{6,1},{7,0},{8,15},{9,14},{10,... | collective-permute-start | bytes 196616 | tf_op jit(solution)/shard_map/ppermute | solution.py:358
  64.4 13.1 %collective-permute-start.4 = (bf16[16,2048]{1,0:T(8,128)(2,1)}, bf16[16,2048]{1,0:T(8,128)(2,1)S(1)}, u32[]{:S(2)}, u32[]{:S(2)}) collective-permute-start(bf16[16,2048]{1,0:T(8,128)(2,1)} %get-tuple-element.40), channel_id=1, source_target_pairs={{0,9},{1,8},{2,11},{3,10},{4,13},{5,12},{6,15},{7,14},{8,1},{9,0},... | collective-permute-start | bytes 196616 | tf_op jit(solution)/shard_map/ppermute | solution.py:358
  66.5 11.0 %collective-permute-start.5 = (bf16[16,2048]{1,0:T(8,128)(2,1)}, bf16[16,2048]{1,0:T(8,128)(2,1)S(1)}, u32[]{:S(2)}, u32[]{:S(2)}) collective-permute-start(bf16[16,2048]{1,0:T(8,128)(2,1)} %get-tuple-element.41), channel_id=1, source_target_pairs={{0,11},{1,10},{2,9},{3,8},{4,15},{5,14},{6,13},{7,12},{8,3},{9,2},... | collective-permute-start | bytes 196616 | tf_op jit(solution)/shard_map/ppermute | solution.py:358
  68.6 8.9 %collective-permute-start.6 = (bf16[16,2048]{1,0:T(8,128)(2,1)S(1)}, bf16[16,2048]{1,0:T(8,128)(2,1)S(1)}, u32[]{:S(2)}, u32[]{:S(2)}) collective-permute-start(bf16[16,2048]{1,0:T(8,128)(2,1)S(1)} %copy-done.3), channel_id=1, source_target_pairs={{0,13},{1,12},{2,15},{3,14},{4,9},{5,8},{6,11},{7,10},{8,5},{9,4},... | collective-permute-start | bytes 196616 | tf_op jit(solution)/shard_map/ppermute | solution.py:358
  71.9 5.6 %collective-permute-start.7 = (bf16[16,2048]{1,0:T(8,128)(2,1)S(1)}, bf16[16,2048]{1,0:T(8,128)(2,1)S(1)}, u32[]{:S(2)}, u32[]{:S(2)}) collective-permute-start(bf16[16,2048]{1,0:T(8,128)(2,1)S(1)} %copy-done.2), channel_id=1, source_target_pairs={{0,15},{1,14},{2,13},{3,12},{4,11},{5,10},{6,9},{7,8},{8,7},{9,6},... | collective-permute-start | bytes 196616 | tf_op jit(solution)/shard_map/ppermute | solution.py:358
  72.3 2.2 %copy-start = (bf16[1,1024,2048]{2,1,0:T(8,128)(2,1)S(1)}, bf16[1,1024,2048]{2,1,0:T(8,128)(2,1)}, u32[]{:S(2)}) copy-start(bf16[1,1024,2048]{2,1,0:T(8,128)(2,1)} %param.12) | copy-start | bytes 12582916
  74.5 2.2 %copy-start.1 = (bf16[1,2048,1024]{2,1,0:T(8,128)(2,1)S(1)}, bf16[1,2048,1024]{2,1,0:T(8,128)(2,1)}, u32[]{:S(2)}) copy-start(bf16[1,2048,1024]{2,1,0:T(8,128)(2,1)} %param.13) | copy-start | bytes 12582916

commit v3 on v2

--- a/solution.py
+++ b/solution.py
@@ -50,14 +50,16 @@
     own_repeat = lax.axis_index("rep")
     own_group = lax.axis_index("grp")
     row = lax.broadcasted_iota(jnp.int32, (capacity, lanes), 0)
+    all_ids = ids[...].astype(jnp.float32)
+    slot_row = lax.broadcasted_iota(jnp.int32, (capacity, all_ids.shape[1]), 0)
+    place = lax.broadcasted_iota(jnp.int32, (capacity, all_ids.shape[1]), 1)
     for step in range(groups):
         group = partner(own_group, step, groups, 1)
         start = pl.multiple_of(group * capacity, capacity)
         live = counts[0, group]
-        tags = jnp.full((capacity, lanes), task_count, jnp.int32)
-        for slot in range(capacity):
-            tags = jnp.where(row == slot, ids[start + slot], tags)
-        tags = jnp.where(row < live, tags, task_count)
+        picked = jnp.where(place == slot_row + start, all_ids, 0.0)
+        tags = jnp.sum(picked, axis=1, keepdims=True)
+        tags = jnp.where(row < live, jnp.broadcast_to(tags, row.shape), task_count)
         rows = pl.ds(start, capacity)
         for hop in range(repeats):
             expert = lax.rem(own_repeat + hop, repeats) * groups + group
@@ -85,10 +87,10 @@
     outs = pl.pallas_call(
         functools.partial(pack_kernel, repeats, groups, capacity),
         out_shape=out_shape,
-        in_specs=[smem_spec, smem_spec, smem_spec, vmem_spec, vmem_spec],
+        in_specs=[vmem_spec, smem_spec, smem_spec, vmem_spec, vmem_spec],
         out_specs=[vmem_spec] * len(out_shape),
         name="pack_blocks",
-    )(task_ids, group_counts, task_gate, inputs, cotangent)
+    )(task_ids.reshape(1, -1), group_counts, task_gate, inputs, cotangent)
     return outs[0], outs[1:]
 
 
@@ -357,7 +359,7 @@
     near_other = [
         lax.ppermute(near[step], ("grp", "dp"), across(turn, step))
         for turn in range(1, halves)
-        for step in range(groups)
+        for step in reversed(range(groups))
     ]
     own = own_rows.reshape(repeats * groups * capacity, width)
     *own_kept, row_grads, far_rows = own_parts(repeats, halves, own, first_weight, second_weight)

time: 86.2 us -> 81.1 us (0.941); the launches traced: 85.8 us -> 79.7 us
  starting transfers between devices: 18 us -> 14.8 us
  waiting for transfers between devices: 11.9 us -> 9.01 us
    ppermute x8, starting transfers between devices: 12.3 us -> 9.09 us  [on_device(): lax.ppermute(near[step], ('grp', 'dp'), across(turn, step))]
    ppermute x8, waiting for transfers between devices: 11.9 us -> 9.01 us  [on_device(): lax.ppermute(near[step], ('grp', 'dp'), across(turn, step))]
  transfers between devices with their start and end apart: 10 -> 10, of which waited for: 1 -> 3; matrix products, arithmetic and copies ran while one was open for 0% -> 0% of each run, Pallas kernels for 9% -> 10%
where the time goes in v3:
time: 81.1 us; the launch traced here: 79.7 us
  blocking collectives  32.6 us (40%)
  Pallas kernels  17.3 us (21%)
  starting transfers between devices  14.8 us (18%)
  waiting for transfers between devices  9.01 us (11%)
  local copies, waits for them, and re-layouts  4.38 us (5%)
  other arithmetic  0.88 us (1%)
    all_to_all x1, blocking collectives, on_device(): own_rows = lax.all_to_all(outgoing, ('rep', 'grp'), 0, 0)  32.6 us
    ppermute x8, starting transfers between devices, on_device(): lax.ppermute(near[step], ('grp', 'dp'), across(turn, step))  9.09 us
    ppermute x8, waiting for transfers between devices, on_device(): lax.ppermute(near[step], ('grp', 'dp'), across(turn, step))  9.01 us
    pallas_call x1, Pallas kernels, rest_parts(): pl.pallas_call(functools.partial(rest_kernel, len(others)), out_shape=[ja...  7.34 us
    pallas_call x1, Pallas kernels, own_parts(): pl.pallas_call(functools.partial(own_kernel, repeats, halves), out_shape=...  6.79 us
    all_to_all x1, starting transfers between devices, on_device(): lax.all_to_all(row_grads.reshape(repeats * groups, capacity, model_width)...  4.49 us
    unnamed x8, local copies, waits for them, and re-layouts  4.38 us
    pallas_call x1, Pallas kernels, pack_blocks(): pl.pallas_call(functools.partial(pack_kernel, repeats, groups, capacity),...  2.38 us
  transfers between devices with their start and end apart: 10, of which 3 were waited for; matrix products, arithmetic and copies ran while one was open for 0% of the time, Pallas kernels for 10%

profile of v3, /device:TPU:1, one launch (start us, length us, event | category | flops | bytes accessed | tf_op | source)
XLA Modules:
  0.0 79.7 jit_solution(6930552720351097644)
XLA Ops:
  0.6 2.4 %pack_blocks.1 = (bf16[16,16,2048]{2,1,0:T(8,128)(2,1)}, bf16[16,2048]{1,0:T(8,128)(2,1)}, bf16[16,2048]{1,0:T(8,128)(2,1)}, bf16[16,2048]{1,0:T(8,128)(2,1)}, b...) custom-call(s32[1,128]{1,0:T(1,128)} %bitcast.19, ...), custom_call_target="tpu_custom_call" | custom-call | tf_op jit(solution)/shard_map/pack_blocks/pallas_call | solution.py:87
  3.0 32.6 %all_to_all.10 = bf16[16,16,2048]{2,1,0:T(8,128)(2,1)S(1)} all-to-all(bf16[16,16,2048]{2,1,0:T(8,128)(2,1)} %get-tuple-element.26), channel_id=1, replica_groups=mesh['rep'=2,'grp'=8,'dp'=2] {'rep','grp'}, dimensions={0} | all-to-all | bytes 2097152 | tf_op jit(solution)/shard_map/all_to_all | solution.py:358
  35.6 6.8 %own_parts.1 = (bf16[256,1024]{1,0:T(8,128)(2,1)S(1)}, bf16[256,2048]{1,0:T(8,128)(2,1)S(1)}, bf16[256,512]{1,0:T(8,128)(2,1)S(1)}, bf16[256,1024]{1,0:T(8,128)(...) custom-call(bf16[256,2048]{1,0:T(8,128)(2,1)S(1)} %bitcast.16, bf16[1024,2048]{1,0:T(8,128)(2,1)} %bitcast.12, ...), custom_call_target="tpu_custom_call" | custom-call | flops 3221225472 | bytes 8388608 | tf_op jit(solution)/shard_map/own_parts/pallas_call | solution.py:194
  42.4 4.5 %all-to-all-start.1 = ((bf16[16,16,1024]{2,1,0:T(8,128)(2,1)}), bf16[16,16,1024]{2,1,0:T(8,128)(2,1)S(1)}, u32[]{:S(2)}, u32[]{:S(2)}) async-start(bf16[16,16,1024]{2,1,0:T(8,128)(2,1)} %bitcast.4), calls=%async_computation.1 | async-start | bytes 1048576 | tf_op jit(solution)/shard_map/all_to_all | solution.py:371
  46.9 1.3 %collective-permute-start.8 = (bf16[128,2048]{1,0:T(8,128)(2,1)S(1)}, bf16[128,2048]{1,0:T(8,128)(2,1)S(1)}, u32[]{:S(2)}, u32[]{:S(2)}) collective-permute-start(bf16[128,2048]{1,0:T(8,128)(2,1)S(1)} %bitcast.17), channel_id=1, source_target_pairs={{0,1},{1,0},{2,3},{3,2},{4,5},{5,4},{6,7},{7,6},{8,9},{9,8},{10,11... | collective-permute-start | bytes 1572872 | tf_op jit(solution)/shard_map/ppermute | solution.py:370
  48.1 2.7 %collective-permute-start = (bf16[16,2048]{1,0:T(8,128)(2,1)}, bf16[16,2048]{1,0:T(8,128)(2,1)S(1)}, u32[]{:S(2)}, u32[]{:S(2)}) collective-permute-start(bf16[16,2048]{1,0:T(8,128)(2,1)} %get-tuple-element.36), channel_id=1, source_target_pairs={{0,15},{1,14},{2,13},{3,12},{4,11},{5,10},{6,9},{7,8},{8,7},{9,6},... | collective-permute-start | bytes 196616 | tf_op jit(solution)/shard_map/ppermute | solution.py:360
  50.9 0.9 %collective-permute-start.1 = (bf16[16,2048]{1,0:T(8,128)(2,1)}, bf16[16,2048]{1,0:T(8,128)(2,1)S(1)}, u32[]{:S(2)}, u32[]{:S(2)}) collective-permute-start(bf16[16,2048]{1,0:T(8,128)(2,1)} %get-tuple-element.37), channel_id=1, source_target_pairs={{0,13},{1,12},{2,15},{3,14},{4,9},{5,8},{6,11},{7,10},{8,5},{9,4},... | collective-permute-start | bytes 196616 | tf_op jit(solution)/shard_map/ppermute | solution.py:360
  51.7 1.5 %collective-permute-start.2 = (bf16[16,2048]{1,0:T(8,128)(2,1)}, bf16[16,2048]{1,0:T(8,128)(2,1)S(1)}, u32[]{:S(2)}, u32[]{:S(2)}) collective-permute-start(bf16[16,2048]{1,0:T(8,128)(2,1)} %get-tuple-element.38), channel_id=1, source_target_pairs={{0,11},{1,10},{2,9},{3,8},{4,15},{5,14},{6,13},{7,12},{8,3},{9,2},... | collective-permute-start | bytes 196616 | tf_op jit(solution)/shard_map/ppermute | solution.py:360
  53.2 1.1 %collective-permute-start.3 = (bf16[16,2048]{1,0:T(8,128)(2,1)}, bf16[16,2048]{1,0:T(8,128)(2,1)S(1)}, u32[]{:S(2)}, u32[]{:S(2)}) collective-permute-start(bf16[16,2048]{1,0:T(8,128)(2,1)} %get-tuple-element.39), channel_id=1, source_target_pairs={{0,9},{1,8},{2,11},{3,10},{4,13},{5,12},{6,15},{7,14},{8,1},{9,0},... | collective-permute-start | bytes 196616 | tf_op jit(solution)/shard_map/ppermute | solution.py:360
  54.3 5.5 %collective-permute-done.refs_0_ = bf16[16,2048]{1,0:T(8,128)(2,1)S(1)} collective-permute-done((bf16[16,2048]{1,0:T(8,128)(2,1)}, bf16[16,2048]{1,0:T(8,128)(2,1)S(1)}, u32[]{:S(2)}, u32[]{:S(2)}) %collective-permute-start) | collective-permute-done | bytes 65568 | tf_op jit(solution)/shard_map/ppermute | solution.py:360
  59.9 0.8 %collective-permute-start.4 = (bf16[16,2048]{1,0:T(8,128)(2,1)}, bf16[16,2048]{1,0:T(8,128)(2,1)S(1)}, u32[]{:S(2)}, u32[]{:S(2)}) collective-permute-start(bf16[16,2048]{1,0:T(8,128)(2,1)} %get-tuple-element.40), channel_id=1, source_target_pairs={{0,7},{1,6},{2,5},{3,4},{4,3},{5,2},{6,1},{7,0},{8,15},{9,14},{10,... | collective-permute-start | bytes 196616 | tf_op jit(solution)/shard_map/ppermute | solution.py:360
  60.7 0.8 %collective-permute-start.5 = (bf16[16,2048]{1,0:T(8,128)(2,1)}, bf16[16,2048]{1,0:T(8,128)(2,1)S(1)}, u32[]{:S(2)}, u32[]{:S(2)}) collective-permute-start(bf16[16,2048]{1,0:T(8,128)(2,1)} %get-tuple-element.41), channel_id=1, source_target_pairs={{0,5},{1,4},{2,7},{3,6},{4,1},{5,0},{6,3},{7,2},{8,13},{9,12},{10,... | collective-permute-start | bytes 196616 | tf_op jit(solution)/shard_map/ppermute | solution.py:360
  61.5 3.1 %collective-permute-done.2.refs_2_ = bf16[16,2048]{1,0:T(8,128)(2,1)S(1)} collective-permute-done((bf16[16,2048]{1,0:T(8,128)(2,1)}, bf16[16,2048]{1,0:T(8,128)(2,1)S(1)}, u32[]{:S(2)}, u32[]{:S(2)}) %collective-permute-start.2) | collective-permute-done | bytes 65568 | tf_op jit(solution)/shard_map/ppermute | solution.py:360
  64.6 0.8 collective-permute-start.6
  65.4 0.5 collective-permute-start.7
  65.9 2.2 %copy-done = bf16[1,1024,2048]{2,1,0:T(8,128)(2,1)S(1)} copy-done((bf16[1,1024,2048]{2,1,0:T(8,128)(2,1)S(1)}, bf16[1,1024,2048]{2,1,0:T(8,128)(2,1)}, u32[]{:S(2)}) %copy-start) | copy-done | bytes 4194328
  68.1 2.2 %copy-done.1 = bf16[1,2048,1024]{2,1,0:T(8,128)(2,1)S(1)} copy-done((bf16[1,2048,1024]{2,1,0:T(8,128)(2,1)S(1)}, bf16[1,2048,1024]{2,1,0:T(8,128)(2,1)}, u32[]{:S(2)}) %copy-start.1) | copy-done | bytes 4194328
  70.3 0.8 stage.1
  71.0 0.0 collective-permute-done.4.refs_4_
  71.1 0.0 collective-permute-done.6.refs_6_
  71.1 0.3 collective-permute-done.7.refs_7_
  71.4 7.3 %rest_parts.1 = (f32[512,2048]{1,0:T(8,128)}, f32[1024,1024]{1,0:T(8,128)}) custom-call(bf16[256,1024]{1,0:T(8,128)(2,1)S(1)} %get-tuple-element.32.act_ref, bf16[256,2048]{1,0:T(8,128)(2,1)S(1)} %get-tuple-element.33.pre_ref, bf16[256,512]{1,0:T(8,128)(2,1)S(1)} %get-tuple-element.34.x_ref, bf16[256,1024]{1,0:T(8,128)(2,1)S(1)} %get-tuple-element.35.scaled_ref, ...), custom_call_target="tpu_custom_call" | custom-call | flops 4294967296 | bytes 8388608 | tf_op jit(solution)/shard_map/rest_parts/pallas_call | solution.py:308
  78.8 0.0 all-to-all-done.1
  78.8 0.9 %convert_reduce_fusion = f32[128,1024]{1,0:T(8,128)} fusion(bf16[2,128,1024]{2,1,0:T(8,128)(2,1)S(1)} %bitcast.18), kind=kLoop, calls=%fused_computation | loop fusion | flops 393216 | bytes 1048576 | tf_op jit(solution)/shard_map/reduce_sum | solution.py:378
  (10 shorter events, 0.0 us)
Async XLA Ops:
  35.6 29.0 %copy-start.3 = (bf16[16,2048]{1,0:T(8,128)(2,1)S(1)}, bf16[16,2048]{1,0:T(8,128)(2,1)}, u32[]{:S(2)}) copy-start(bf16[16,2048]{1,0:T(8,128)(2,1)} %get-tuple-element.42) | copy-start | bytes 196612
  35.6 29.8 %copy-start.2 = (bf16[16,2048]{1,0:T(8,128)(2,1)S(1)}, bf16[16,2048]{1,0:T(8,128)(2,1)}, u32[]{:S(2)}) copy-start(bf16[16,2048]{1,0:T(8,128)(2,1)} %get-tuple-element.43) | copy-start | bytes 196612
  42.4 36.4 %all-to-all-start.1 = ((bf16[16,16,1024]{2,1,0:T(8,128)(2,1)}), bf16[16,16,1024]{2,1,0:T(8,128)(2,1)S(1)}, u32[]{:S(2)}, u32[]{:S(2)}) async-start(bf16[16,16,1024]{2,1,0:T(8,128)(2,1)} %bitcast.4), calls=%async_computation.1 | async-start | bytes 1048576 | tf_op jit(solution)/shard_map/all_to_all | solution.py:371
  46.9 24.6 %collective-permute-start.8 = (bf16[128,2048]{1,0:T(8,128)(2,1)S(1)}, bf16[128,2048]{1,0:T(8,128)(2,1)S(1)}, u32[]{:S(2)}, u32[]{:S(2)}) collective-permute-start(bf16[128,2048]{1,0:T(8,128)(2,1)S(1)} %bitcast.17), channel_id=1, source_target_pairs={{0,1},{1,0},{2,3},{3,2},{4,5},{5,4},{6,7},{7,6},{8,9},{9,8},{10,11... | collective-permute-start | bytes 1572872 | tf_op jit(solution)/shard_map/ppermute | solution.py:370
  48.1 11.7 %collective-permute-start = (bf16[16,2048]{1,0:T(8,128)(2,1)}, bf16[16,2048]{1,0:T(8,128)(2,1)S(1)}, u32[]{:S(2)}, u32[]{:S(2)}) collective-permute-start(bf16[16,2048]{1,0:T(8,128)(2,1)} %get-tuple-element.36), channel_id=1, source_target_pairs={{0,15},{1,14},{2,13},{3,12},{4,11},{5,10},{6,9},{7,8},{8,7},{9,6},... | collective-permute-start | bytes 196616 | tf_op jit(solution)/shard_map/ppermute | solution.py:360
  50.9 9.8 %collective-permute-start.1 = (bf16[16,2048]{1,0:T(8,128)(2,1)}, bf16[16,2048]{1,0:T(8,128)(2,1)S(1)}, u32[]{:S(2)}, u32[]{:S(2)}) collective-permute-start(bf16[16,2048]{1,0:T(8,128)(2,1)} %get-tuple-element.37), channel_id=1, source_target_pairs={{0,13},{1,12},{2,15},{3,14},{4,9},{5,8},{6,11},{7,10},{8,5},{9,4},... | collective-permute-start | bytes 196616 | tf_op jit(solution)/shard_map/ppermute | solution.py:360
  51.7 12.9 %collective-permute-start.2 = (bf16[16,2048]{1,0:T(8,128)(2,1)}, bf16[16,2048]{1,0:T(8,128)(2,1)S(1)}, u32[]{:S(2)}, u32[]{:S(2)}) collective-permute-start(bf16[16,2048]{1,0:T(8,128)(2,1)} %get-tuple-element.38), channel_id=1, source_target_pairs={{0,11},{1,10},{2,9},{3,8},{4,15},{5,14},{6,13},{7,12},{8,3},{9,2},... | collective-permute-start | bytes 196616 | tf_op jit(solution)/shard_map/ppermute | solution.py:360
  53.2 12.2 %collective-permute-start.3 = (bf16[16,2048]{1,0:T(8,128)(2,1)}, bf16[16,2048]{1,0:T(8,128)(2,1)S(1)}, u32[]{:S(2)}, u32[]{:S(2)}) collective-permute-start(bf16[16,2048]{1,0:T(8,128)(2,1)} %get-tuple-element.39), channel_id=1, source_target_pairs={{0,9},{1,8},{2,11},{3,10},{4,13},{5,12},{6,15},{7,14},{8,1},{9,0},... | collective-permute-start | bytes 196616 | tf_op jit(solution)/shard_map/ppermute | solution.py:360
  59.9 11.2 %collective-permute-start.4 = (bf16[16,2048]{1,0:T(8,128)(2,1)}, bf16[16,2048]{1,0:T(8,128)(2,1)S(1)}, u32[]{:S(2)}, u32[]{:S(2)}) collective-permute-start(bf16[16,2048]{1,0:T(8,128)(2,1)} %get-tuple-element.40), channel_id=1, source_target_pairs={{0,7},{1,6},{2,5},{3,4},{4,3},{5,2},{6,1},{7,0},{8,15},{9,14},{10,... | collective-permute-start | bytes 196616 | tf_op jit(solution)/shard_map/ppermute | solution.py:360
  60.7 10.4 %collective-permute-start.5 = (bf16[16,2048]{1,0:T(8,128)(2,1)}, bf16[16,2048]{1,0:T(8,128)(2,1)S(1)}, u32[]{:S(2)}, u32[]{:S(2)}) collective-permute-start(bf16[16,2048]{1,0:T(8,128)(2,1)} %get-tuple-element.41), channel_id=1, source_target_pairs={{0,5},{1,4},{2,7},{3,6},{4,1},{5,0},{6,3},{7,2},{8,13},{9,12},{10,... | collective-permute-start | bytes 196616 | tf_op jit(solution)/shard_map/ppermute | solution.py:360
  64.6 6.5 %collective-permute-start.6 = (bf16[16,2048]{1,0:T(8,128)(2,1)S(1)}, bf16[16,2048]{1,0:T(8,128)(2,1)S(1)}, u32[]{:S(2)}, u32[]{:S(2)}) collective-permute-start(bf16[16,2048]{1,0:T(8,128)(2,1)S(1)} %copy-done.3), channel_id=1, source_target_pairs={{0,3},{1,2},{2,1},{3,0},{4,7},{5,6},{6,5},{7,4},{8,11},{9,10},{10,... | collective-permute-start | bytes 196616 | tf_op jit(solution)/shard_map/ppermute | solution.py:360
  65.4 6.0 %collective-permute-start.7 = (bf16[16,2048]{1,0:T(8,128)(2,1)S(1)}, bf16[16,2048]{1,0:T(8,128)(2,1)S(1)}, u32[]{:S(2)}, u32[]{:S(2)}) collective-permute-start(bf16[16,2048]{1,0:T(8,128)(2,1)S(1)} %copy-done.2), channel_id=1, source_target_pairs={{0,1},{1,0},{2,3},{3,2},{4,5},{5,4},{6,7},{7,6},{8,9},{9,8},{10,11... | collective-permute-start | bytes 196616 | tf_op jit(solution)/shard_map/ppermute | solution.py:360
  65.9 2.2 %copy-start = (bf16[1,1024,2048]{2,1,0:T(8,128)(2,1)S(1)}, bf16[1,1024,2048]{2,1,0:T(8,128)(2,1)}, u32[]{:S(2)}) copy-start(bf16[1,1024,2048]{2,1,0:T(8,128)(2,1)} %param.12) | copy-start | bytes 12582916
  68.1 2.2 %copy-start.1 = (bf16[1,2048,1024]{2,1,0:T(8,128)(2,1)S(1)}, bf16[1,2048,1024]{2,1,0:T(8,128)(2,1)}, u32[]{:S(2)}) copy-start(bf16[1,2048,1024]{2,1,0:T(8,128)(2,1)} %param.13) | copy-start | bytes 12582916
